TPU v7x, 1024 devices: a whole 4x4x32 slice. The times are simulated.
1024 devices in a mesh: group: 2 (over core), rep: 32 (over x, z_lo), tp: 16 (over y, z_hi).
Axes of the slice: x: 4, y: 4, z: 32 (z_hi: 4, z_lo: 8; z = z_hi * 8 + z_lo), core: 2. Of those that a mesh axis runs over, the one named last changes fastest.
Arguments:
- master_weight: float32 [8192, 1024], P(('group', 'rep', 'tp')), may hold values from -0.25 to 0.25
- grad: float32 [8192, 1024], P(('group', 'rep', 'tp')), may hold values from -0.015625 to 0.015625
- moment1: float32 [8192, 1024], P(('group', 'rep', 'tp')), may hold values from -0.015625 to 0.015625
- moment2: float32 [8192, 1024], P(('group', 'rep', 'tp')), may hold values from 1e-08 to 1e-06
- step_count: int32 [1], replicated, may hold values from 1 to 299
- x_new: bfloat16 [4, 256, 8192], P(None, ('group', 'rep')), may hold values from -6 to 6
- queries: bfloat16 [4, 256, 8192], P(None, ('group', 'rep')), may hold values from -132 to 132
- new_keys: bfloat16 [4, 256, 1024], P(None, ('group', 'rep')), may hold values from -6 to 6
- cache_keys: bfloat16 [256, 1024, 1024], P(('group', 'rep'), 'tp'), may hold values from -6 to 6
- cache_values: bfloat16 [256, 1024, 1024], P(('group', 'rep'), 'tp'), may hold values from -6 to 6
- lengths: int32 [64, 4], P(('group', 'rep')), may hold values from 1 to 1024, 2560 in all within a row
Outputs:
- new_weight: float32 [8192, 1024], P(('group', 'rep', 'tp'))
- channel_scale: float32 [1024], P('tp')
- fresh_values: bfloat16 [4, 256, 1024], P(None, ('group', 'rep'), 'tp')
- attention: float32 [4, 256, 8192], P(None, ('group', 'rep'), 'tp')
Inputs may be any that keep to these rules, and one draw needn't show every extreme that they name: `lengths`: within each replica's 4 sequences at least one has exactly 1024 live positions.
All inputs are finite; a program needn't handle non-finite values.
Results may differ from a plain program's by a relative error of at most 0.0055.
Values may be sent and summed in bfloat16 or wider, within the bound.
A program may use at most 64 MiB of HBM per device.

v0:
```python
import math

import jax
import jax.numpy as jnp
from jax import lax
from jax.sharding import PartitionSpec as P

H = 64
KV = 8
HD = 128


beta_first = 0.9
beta_second = 0.999
learn_rate = 0.01
decay_rate = 0.1
adam_floor = 1e-08
scale_floor = 1e-06
code_range = 448.0
masked_score = -1e30


def joined_along(blocks, dim):
    shape = list(blocks.shape[1:])
    shape[dim] *= blocks.shape[0]
    return jnp.moveaxis(blocks, 0, dim).reshape(shape)


def sent_to_all(array, axis):
    peers = lax.axis_size(axis)
    return lax.all_to_all(
        jnp.broadcast_to(array[None], (peers, *array.shape)), axis, 0, 0, tiled=True
    )


def gather_directly(array, axis, dim):
    return joined_along(sent_to_all(array, axis), dim)


def adamw(master_weight, grad, moment1, moment2, step_count):
    steps_done = step_count[0].astype(jnp.float32)
    first = beta_first * moment1 + (1.0 - beta_first) * grad
    second = beta_second * moment2 + (1.0 - beta_second) * grad * grad
    correction = jnp.sqrt(1.0 - jnp.exp(steps_done * math.log(beta_second))) / (
        1.0 - jnp.exp(steps_done * math.log(beta_first))
    )
    return (
        master_weight
        - learn_rate * correction * first / (jnp.sqrt(second) + adam_floor)
        - learn_rate * decay_rate * master_weight
    )


def body(
    master_weight,
    grad,
    moment1,
    moment2,
    step_count,
    x_new,
    queries,
    new_keys,
    cache_keys,
    cache_values,
    lengths,
):
    new_weight = adamw(master_weight, grad, moment1, moment2, step_count)
    tp_count = lax.axis_size("tp")
    tp_index = lax.axis_index("tp")
    moved = lax.all_to_all(new_weight, "tp", split_axis=1, concat_axis=0, tiled=True)
    gathered = lax.all_gather(moved, ("group", "rep"), axis=0, tiled=True)
    scale_own = (jnp.max(jnp.abs(gathered), axis=0) + scale_floor) / code_range
    quant = (gathered / scale_own).astype(jnp.bfloat16)
    steps_count, batch_rows = (queries.shape[0], queries.shape[1])
    flat = x_new.reshape(steps_count * batch_rows, x_new.shape[2])
    value_own = (jnp.dot(flat, quant, preferred_element_type=jnp.float32) * scale_own).astype(
        jnp.bfloat16
    )
    value_all = gather_directly(value_own, "tp", 1)
    group_size = H // KV
    local_len = cache_keys.shape[1]
    inverse = 1.0 / math.sqrt(HD)
    query_grid = queries.reshape(steps_count, batch_rows, KV, group_size, HD).transpose(
        1, 2, 3, 0, 4
    )
    key_grid = cache_keys.reshape(batch_rows, local_len, KV, HD)
    value_grid = cache_values.reshape(batch_rows, local_len, KV, HD)
    scores = (
        jnp.einsum("bkgsd,bpkd->bkgsp", query_grid, key_grid, preferred_element_type=jnp.float32)
        * inverse
    )
    positions = tp_index * local_len + jnp.arange(local_len, dtype=jnp.int32)
    live = (positions[None, :] < lengths[0][:, None])[:, None, None, None, :]
    masked = jnp.where(live, scores, masked_score)
    peak_local = jnp.max(masked, axis=-1)
    weights = jnp.where(live, jnp.exp(masked - peak_local[..., None]), 0.0)
    sum_local = jnp.sum(weights, axis=-1)
    part_local = jnp.einsum(
        "bkgsp,bpkd->bkgsd",
        weights.astype(jnp.bfloat16),
        value_grid,
        preferred_element_type=jnp.float32,
    )
    peak_local = peak_local.reshape(batch_rows, H, steps_count)
    sum_local = sum_local.reshape(batch_rows, H, steps_count)
    part_local = part_local.reshape(batch_rows, H, steps_count, HD)
    own_heads = H // tp_count
    head_start = tp_index * own_heads
    peak_set, sum_set, part_set = (
        lax.all_to_all(peak_local[None], "tp", split_axis=2, concat_axis=0, tiled=True),
        lax.all_to_all(sum_local[None], "tp", split_axis=2, concat_axis=0, tiled=True),
        lax.all_to_all(part_local[None], "tp", split_axis=2, concat_axis=0, tiled=True),
    )
    own_peak = jnp.max(peak_set, axis=0)
    factors = jnp.exp(peak_set - own_peak[None])
    own_sum = jnp.sum(sum_set * factors, axis=0)
    own_part = jnp.sum(part_set * factors[..., None], axis=0)
    query_heads = lax.dynamic_slice_in_dim(
        query_grid.reshape(batch_rows, H, steps_count, HD), head_start, own_heads, 1
    )
    fresh_keys = jnp.repeat(
        new_keys.reshape(steps_count, batch_rows, KV, HD).transpose(1, 2, 0, 3), group_size, axis=1
    )
    fresh_keys = lax.dynamic_slice_in_dim(fresh_keys, head_start, own_heads, 1)
    fresh_vals = jnp.repeat(
        value_all.reshape(steps_count, batch_rows, KV, HD).transpose(1, 2, 0, 3), group_size, axis=1
    )
    fresh_vals = lax.dynamic_slice_in_dim(fresh_vals, head_start, own_heads, 1)
    fresh_scores = (
        jnp.einsum("bhsd,bhjd->bhsj", query_heads, fresh_keys, preferred_element_type=jnp.float32)
        * inverse
    )
    causal = (
        jnp.arange(steps_count, dtype=jnp.int32)[:, None]
        >= jnp.arange(steps_count, dtype=jnp.int32)[None, :]
    )
    peak_score = jnp.maximum(
        own_peak, jnp.max(jnp.where(causal, fresh_scores, masked_score), axis=-1)
    )
    factor = jnp.exp(own_peak - peak_score)
    fresh_weights = jnp.where(causal, jnp.exp(fresh_scores - peak_score[..., None]), 0.0)
    denominator = own_sum * factor + jnp.sum(fresh_weights, axis=-1)
    mixed = own_part * factor[..., None] + jnp.einsum(
        "bhsj,bhjd->bhsd",
        fresh_weights.astype(jnp.bfloat16),
        fresh_vals,
        preferred_element_type=jnp.float32,
    )
    result = mixed / denominator[..., None]
    attention = result.transpose(2, 0, 1, 3).reshape(steps_count, batch_rows, own_heads * HD)
    fresh_out = value_own.reshape(steps_count, batch_rows, value_own.shape[1])
    return (new_weight, scale_own, fresh_out, attention)


def solution(mesh):
    return jax.shard_map(
        body,
        mesh=mesh,
        in_specs=(
            P(("group", "rep", "tp"), None),
            P(("group", "rep", "tp"), None),
            P(("group", "rep", "tp"), None),
            P(("group", "rep", "tp"), None),
            P(),
            P(None, ("group", "rep"), None),
            P(None, ("group", "rep"), None),
            P(None, ("group", "rep"), None),
            P(("group", "rep"), "tp", None),
            P(("group", "rep"), "tp", None),
            P(("group", "rep"), None),
        ),
        out_specs=(
            P(("group", "rep", "tp"), None),
            P("tp"),
            P(None, ("group", "rep"), "tp"),
            P(None, ("group", "rep"), "tp"),
        ),
        check_vma=False,
    )
```

profile of v0, /device:TPU:1, one launch (start us, length us, event | category | flops | bytes accessed | tf_op | source)
XLA Modules:
  0.0 288.0 jit_solution(1004899404969647204)
XLA Ops:
  8.0 0.8 fusion.21
  8.9 0.1 all_to_all.56
  9.0 0.7 reshape.132
  9.7 31.6 %all-to-all-start = ((f32[16,1,512]{2,1,0:T(1,128)}), f32[16,1,512]{2,1,0:T(1,128)S(1)}, u32[]{:S(2)}, u32[]{:S(2)}) async-start(f32[16,1,512]{2,1,0:T(1,128)} %reshape.132), calls=%async_computation | async-start | bytes 65536 | tf_op jit(solution)/shard_map/all_to_all | solution.py:70
  41.4 23.2 %all-to-all-done = f32[16,1,512]{2,1,0:T(1,128)S(1)} async-done(((f32[16,1,512]{2,1,0:T(1,128)}), f32[16,1,512]{2,1,0:T(1,128)S(1)}, u32[]{:S(2)}, u32[]{:S(2)}) %all-to-all-start) | async-done | bytes 32800 | tf_op jit(solution)/shard_map/all_to_all | solution.py:70
  64.6 0.5 broadcast.42
  65.1 0.7 reduce.1
  65.9 0.1 reshape.133
  66.0 0.6 bitcast_bitcast_fusion.2
  66.6 0.7 broadcast_compare_fusion
  67.3 1.1 copy.131
  68.5 1.2 reshape.118
  69.8 0.5 fusion.37
  70.3 0.4 fusion.9
  70.7 0.9 copy.127
  71.6 3.5 %all-to-all-start.4 = ((f32[1,4,64,4]{3,1,0,2:T(4,128)}), f32[1,4,64,4]{3,1,0,2:T(4,128)S(1)}, u32[]{:S(2)}, u32[]{:S(2)}) async-start(f32[1,4,64,4]{3,1,0,2:T(4,128)} %bitcast.28), calls=%async_computation.4 | async-start | bytes 262144 | tf_op jit(solution)/shard_map/all_to_all | solution.py:111
  75.1 0.1 copy.132
  75.3 0.9 copy.124
  76.2 26.4 %all-to-all-done.4 = f32[1,4,64,4]{3,1,0,2:T(4,128)S(1)} async-done(((f32[1,4,64,4]{3,1,0,2:T(4,128)}), f32[1,4,64,4]{3,1,0,2:T(4,128)S(1)}, u32[]{:S(2)}, u32[]{:S(2)}) %all-to-all-start.4) | async-done | bytes 4128 | tf_op jit(solution)/shard_map/all_to_all | solution.py:111
  102.6 3.5 %all-to-all-start.2 = ((f32[1,4,64,4]{3,1,0,2:T(4,128)}), f32[1,4,64,4]{3,1,0,2:T(4,128)S(1)}, u32[]{:S(2)}, u32[]{:S(2)}) async-start(f32[1,4,64,4]{3,1,0,2:T(4,128)} %bitcast.13), calls=%async_computation.2 | async-start | bytes 262144 | tf_op jit(solution)/shard_map/all_to_all | solution.py:110
  106.1 0.3 convolution_bitcast_fusion
  106.4 1.1 copy.94
  107.5 25.9 %all-to-all-done.2 = f32[1,4,64,4]{3,1,0,2:T(4,128)S(1)} async-done(((f32[1,4,64,4]{3,1,0,2:T(4,128)}), f32[1,4,64,4]{3,1,0,2:T(4,128)S(1)}, u32[]{:S(2)}, u32[]{:S(2)}) %all-to-all-start.2) | async-done | bytes 4128 | tf_op jit(solution)/shard_map/all_to_all | solution.py:110
  133.4 3.7 %all-to-all-start.1 = ((f32[1,4,64,4,128]{4,3,1,0,2:T(4,128)}), f32[1,4,64,4,128]{4,3,1,0,2:T(4,128)S(1)}, u32[]{:S(2)}, u32[]{:S(2)}) async-start(f32[1,4,64,4,128]{4,3,1,0,2:T(4,128)} %copy.94), calls=%async_computation.1 | async-start | bytes 1048576 | tf_op jit(solution)/shard_map/all_to_all | solution.py:112
  137.1 0.1 reshape.116
  137.2 0.2 copy.100
  137.5 0.1 broadcast_in_dim.60
  137.5 0.2 select_reduce_fusion
  137.7 0.1 copy.102
  137.8 0.5 copy.128
  138.4 0.5 copy.125
  138.9 0.1 copy.105
  139.1 0.1 copy.112
  139.3 89.9 %all-gather.2.cloned.1.call-done = f32[8192,64]{1,0:T(8,128)} async-done(((f32[128,64]{1,0:T(8,128)}), f32[8192,64]{1,0:T(8,128)}) %all-gather.2.cloned.1.call-update) | async-done | bytes 2097168 | tf_op jit(solution)/shard_map/all_gather | solution.py:71
  229.1 3.4 %abs_reduce_fusion = f32[64]{0:T(128)S(1)} fusion(f32[8192,64]{1,0:T(8,128)} %all-gather.2.cloned.1.call-done), kind=kLoop, calls=%fused_computation.1 | loop fusion | flops 1048512 | bytes 2097408 | tf_op jit(solution)/shard_map/reduce_max | solution.py:72
  232.6 0.4 fusion.5
  233.0 0.1 copy-done.6
  233.1 0.7 reshape.134
  233.8 22.8 %all-to-all-start.3 = ((bf16[16,2,512]{2,1,0:T(2,128)(2,1)}), bf16[16,2,512]{2,1,0:T(2,128)(2,1)S(1)}, u32[]{:S(2)}, u32[]{:S(2)}) async-start(bf16[16,2,512]{2,1,0:T(2,128)(2,1)} %reshape.134), calls=%async_computation.3 | async-start | bytes 65536 | tf_op jit(solution)/shard_map/all_to_all | solution.py:31
  256.7 0.1 copy.113
  256.8 0.1 copy.103
  256.9 0.3 fusion.6
  257.3 22.7 %all-to-all-done.3 = bf16[16,2,512]{2,1,0:T(2,128)(2,1)S(1)} async-done(((bf16[16,2,512]{2,1,0:T(2,128)(2,1)}), bf16[16,2,512]{2,1,0:T(2,128)(2,1)S(1)}, u32[]{:S(2)}, u32[]{:S(2)}) %all-to-all-start.3) | async-done | bytes 32800 | tf_op jit(solution)/shard_map/all_to_all | solution.py:31
  280.0 0.1 reshape.135
  280.1 0.1 reshape_reshape.3
  280.2 0.1 broadcast_in_dim.64
  280.3 0.2 fusion.3
  280.6 0.6 reshape.125
  (33 shorter events, 0.5 us)
Async XLA Ops:
  7.2 68.0 %copy-start.1 = (bf16[4,64,1024]{2,1,0:T(8,128)(2,1)S(1)}, bf16[4,64,1024]{2,1,0:T(8,128)(2,1)}, u32[]{:S(2)}) copy-start(bf16[4,64,1024]{2,1,0:T(8,128)(2,1)} %param.20) | copy-start | bytes 1572868
  8.9 67.3 %copy-start.3 = (f32[8,1024]{1,0:T(8,128)}, f32[8,1024]{1,0:T(8,128)S(1)}, u32[]{:S(2)}) copy-start(f32[8,1024]{1,0:T(8,128)S(1)} %fusion.21) | copy-start | bytes 98308
  9.7 54.9 %all-to-all-start = ((f32[16,1,512]{2,1,0:T(1,128)}), f32[16,1,512]{2,1,0:T(1,128)S(1)}, u32[]{:S(2)}, u32[]{:S(2)}) async-start(f32[16,1,512]{2,1,0:T(1,128)} %reshape.132), calls=%async_computation | async-start | bytes 65536 | tf_op jit(solution)/shard_map/all_to_all | solution.py:70
  41.3 187.8 %all-gather.2.cloned.1.call-start = ((), (), s32[]{:S(2)}) async-start(), calls=%async_computation.5 | async-start | bytes 4259840 | tf_op jit(solution)/shard_map/all_gather | solution.py:71
  69.8 67.4 %copy-start.2 = (bf16[4,4,8192]{2,1,0:T(4,128)(2,1)S(1)}, bf16[4,4,8192]{2,1,0:T(4,128)(2,1)}, u32[]{:S(2)}) copy-start(bf16[4,4,8192]{2,1,0:T(4,128)(2,1)} %param.16) | copy-start | bytes 786436
  70.3 66.9 %copy-start.4 = (bf16[4,4,1024]{2,1,0:T(4,128)(2,1)S(1)}, bf16[4,4,1024]{2,1,0:T(4,128)(2,1)}, u32[]{:S(2)}) copy-start(bf16[4,4,1024]{2,1,0:T(4,128)(2,1)} %param.18) | copy-start | bytes 98308
  71.6 31.0 %all-to-all-start.4 = ((f32[1,4,64,4]{3,1,0,2:T(4,128)}), f32[1,4,64,4]{3,1,0,2:T(4,128)S(1)}, u32[]{:S(2)}, u32[]{:S(2)}) async-start(f32[1,4,64,4]{3,1,0,2:T(4,128)} %bitcast.28), calls=%async_computation.4 | async-start | bytes 262144 | tf_op jit(solution)/shard_map/all_to_all | solution.py:111
  102.6 30.8 %all-to-all-start.2 = ((f32[1,4,64,4]{3,1,0,2:T(4,128)}), f32[1,4,64,4]{3,1,0,2:T(4,128)S(1)}, u32[]{:S(2)}, u32[]{:S(2)}) async-start(f32[1,4,64,4]{3,1,0,2:T(4,128)} %bitcast.13), calls=%async_computation.2 | async-start | bytes 262144 | tf_op jit(solution)/shard_map/all_to_all | solution.py:110
  133.4 100.4 %all-to-all-start.1 = ((f32[1,4,64,4,128]{4,3,1,0,2:T(4,128)}), f32[1,4,64,4,128]{4,3,1,0,2:T(4,128)S(1)}, u32[]{:S(2)}, u32[]{:S(2)}) async-start(f32[1,4,64,4,128]{4,3,1,0,2:T(4,128)} %copy.94), calls=%async_computation.1 | async-start | bytes 1048576 | tf_op jit(solution)/shard_map/all_to_all | solution.py:112
  229.1 3.4 %copy-start = (f32[8192,64]{1,0:T(8,128)S(1)}, f32[8192,64]{1,0:T(8,128)}, u32[]{:S(2)}) copy-start(f32[8192,64]{1,0:T(8,128)} %all-gather.2.cloned.1.call-done) | copy-start | bytes 6291460
  232.6 0.5 copy-start.6
  233.1 48.1 %copy-start.5 = (bf16[64,16]{0,1:T(8,128)(2,1)}, bf16[64,16]{0,1:T(8,128)(2,1)S(1)}, u32[]{:S(2)}) copy-start(bf16[64,16]{0,1:T(8,128)(2,1)S(1)} %fusion.5) | copy-start | bytes 6148
  233.8 46.1 %all-to-all-start.3 = ((bf16[16,2,512]{2,1,0:T(2,128)(2,1)}), bf16[16,2,512]{2,1,0:T(2,128)(2,1)S(1)}, u32[]{:S(2)}, u32[]{:S(2)}) async-start(bf16[16,2,512]{2,1,0:T(2,128)(2,1)} %reshape.134), calls=%async_computation.3 | async-start | bytes 65536 | tf_op jit(solution)/shard_map/all_to_all | solution.py:31
Sparse Core Ops, SparseCore 0:
  66.7 162.3 all-gather.1
where the time goes:
time: 291 us; the launch traced here: 288 us
  waiting for transfers between devices  188 us (65%)
  starting transfers between devices  65.2 us (22%)
  between operations  15.2 us (5%)
  local copies, waits for them, and re-layouts  11.3 us (4%)
  other arithmetic  6.69 us (2%)
    all_gather x1, waiting for transfers between devices, body(): gathered = lax.all_gather(moved, ('group', 'rep'), axis=0, tiled=True)  89.9 us
    all_to_all x1, starting transfers between devices, body(): lax.all_to_all(new_weight, 'tp', split_axis=1, concat_axis=0, tiled=True)  31.6 us
    all_to_all x1, waiting for transfers between devices, body(): lax.all_to_all(sum_local[None], 'tp', split_axis=2, concat_axis=0, tiled=...  26.4 us
    all_to_all x1, waiting for transfers between devices, body(): lax.all_to_all(peak_local[None], 'tp', split_axis=2, concat_axis=0, tiled...  25.9 us
    all_to_all x1, waiting for transfers between devices, body(): lax.all_to_all(new_weight, 'tp', split_axis=1, concat_axis=0, tiled=True)  23.2 us
    all_to_all x1, starting transfers between devices, sent_to_all(): lax.all_to_all(jnp.broadcast_to(array[None], (peers, *array.shape)), axis...  22.8 us
    all_to_all x1, waiting for transfers between devices, sent_to_all(): lax.all_to_all(jnp.broadcast_to(array[None], (peers, *array.shape)), axis...  22.7 us
  transfers between devices with their start and end apart: 6, of which 5 were waited for; matrix products, arithmetic and copies ran while one was open for 5% of the time, Pallas kernels for 0%

commit v1 on v0

v1 whole, which is shorter than its diff:
```python
import functools
import math

import jax
import jax.numpy as jnp
from jax import lax
from jax.experimental import pallas as pl
from jax.experimental.pallas import tpu as pltpu
from jax.sharding import PartitionSpec as P

H = 64
KV = 8
HD = 128
STEPS = 4
BR = 4

beta_first = 0.9
beta_second = 0.999
learn_rate = 0.01
decay_rate = 0.1
adam_floor = 1e-08
scale_floor = 1e-06
code_range = 448.0
masked_score = -1e30

F32 = jnp.float32
BF16 = jnp.bfloat16
MESH = pl.DeviceIdType.MESH

NX, NY, ZLO, ZHI = 4, 4, 8, 4
NZ = ZLO * ZHI
WINDOW = (1, -1, 2, -2, 3, -3, 4)


def kernel(
    mw_ref,
    grad_ref,
    m1_ref,
    m2_ref,
    step_ref,
    x_ref,
    q_ref,
    nk_ref,
    k_ref,
    v_ref,
    len_ref,
    nw_ref,
    scale_ref,
    fresh_ref,
    att_ref,
    w_buf,
    xp_buf,
    sel_mat,
    mask_buf,
    ya_buf,
    ys_buf,
    yar_buf,
    ysr_buf,
    za_buf,
    zs_buf,
    zar_buf,
    zsr_buf,
    cs_buf,
    cr_buf,
    yf_buf,
    yfr_buf,
    zf_buf,
    zfr_buf,
    win_send,
    win_recv,
    x_send,
    x_recv,
    xp_sem,
    c_sem,
    y_send,
    y_recv,
    z_send,
    z_recv,
):
    g = lax.axis_index("group")
    rep = lax.axis_index("rep")
    tp = lax.axis_index("tp")
    x, zl = rep // ZLO, rep % ZLO
    y, zh = tp // ZHI, tp % ZHI
    z = zh * ZLO + zl

    def at_z(offset):
        there = (z + offset + NZ) % NZ
        return {"rep": x * ZLO + there % ZLO, "tp": y * ZHI + there // ZLO}

    def at_x(offset):
        return {"rep": ((x + offset + NX) % NX) * ZLO + zl}

    def at_y(offset):
        return {"tp": ((y + offset) % NY) * ZHI + zh}

    partner = {"group": 1 - g}

    barrier = pltpu.get_barrier_semaphore()
    peers = [at_z(d) for d in (8, 24, 16, 4, -4, 3, -3, 2, -2, 1, -1)]
    peers += [at_y(d) for d in (2, 1, 3)] + [at_x(d) for d in (1, -1)] + [partner]
    for peer in peers:
        pl.semaphore_signal(barrier, inc=1, device_id=peer, device_id_type=MESH)

    def remote(src, dst, send, recv, peer):
        return pltpu.make_async_remote_copy(
            src_ref=src, dst_ref=dst, send_sem=send, recv_sem=recv, device_id=peer, device_id_type=MESH
        )

    steps_done = jnp.full((8, 1024), step_ref[0], jnp.int32).astype(F32)
    first = beta_first * m1_ref[...] + (1.0 - beta_first) * grad_ref[...]
    second = beta_second * m2_ref[...] + (1.0 - beta_second) * grad_ref[...] * grad_ref[...]
    correction = jnp.sqrt(1.0 - jnp.exp(steps_done * math.log(beta_second))) / (
        1.0 - jnp.exp(steps_done * math.log(beta_first))
    )
    nw = (
        mw_ref[...]
        - learn_rate * correction * first / (jnp.sqrt(second) + adam_floor)
        - learn_rate * decay_rate * mw_ref[...]
    )
    nw_ref[...] = nw
    w_buf[x, zl] = jnp.concatenate([nw[:, :512], nw[:, 512:]], axis=0).astype(BF16)

    rows_b = []
    lane_b = lax.broadcasted_iota(jnp.int32, (64, 128), 1) % BR
    position = tp * 64 + lax.broadcasted_iota(jnp.int32, (64, 128), 0)
    for b in range(BR):
        live = jnp.logical_and(position < len_ref[0, b], lane_b == b)
        rows_b.append(jnp.where(live, 1.0, 0.0))
    mask_buf[...] = jnp.concatenate(rows_b, axis=0)
    inverse = 1.0 / math.sqrt(HD)

    def attend(kv, carry):
        base = kv * 1024
        queries = jnp.concatenate(
            [q_ref[:, pl.ds(pl.multiple_of(base + h * 128, 128), 128)] for h in range(8)], axis=0
        )
        columns = pl.ds(pl.multiple_of(kv * 128, 128), 128)
        scores = (
            lax.dot_general(
                k_ref[:, columns], queries, (((1,), (1,)), ((), ())), preferred_element_type=F32
            )
            * inverse
        )
        live = mask_buf[...] > 0.5
        masked = jnp.where(live, scores, masked_score)
        peak = jnp.max(masked, axis=0, keepdims=True)
        weights = jnp.where(live, jnp.exp(masked - peak), 0.0)
        total = jnp.sum(weights, axis=0, keepdims=True)
        part = lax.dot_general(
            v_ref[:, columns],
            weights.astype(BF16),
            (((0,), (0,)), ((), ())),
            preferred_element_type=F32,
        )
        ya_buf[kv] = part.astype(BF16)
        row = lax.broadcasted_iota(jnp.int32, (8, 128), 0)
        ys_buf[kv] = jnp.where(row == 0, peak, total)
        return carry

    lax.fori_loop(0, KV, attend, 0)

    for low in range(ZLO):
        there = (z + 28 + (low - z + 4 + NZ) % ZLO) % NZ
        lanes = (y * ZHI + there // ZLO) * 8
        r = lax.broadcasted_iota(jnp.int32, (128, 256), 0)
        c = lax.broadcasted_iota(jnp.int32, (128, 256), 1)
        k = c & 127
        hit = jnp.logical_and(
            jnp.logical_and((k >> 4) == low, ((k >> 3) & 1) == (c >> 7)), r == lanes + (k & 7)
        )
        sel_mat[low * 128 : (low + 1) * 128, :] = jnp.where(hit, 1.0, 0.0).astype(BF16)

    pl.semaphore_wait(barrier, len(peers))

    windows = []
    for i, d in enumerate(WINDOW):
        copy = remote(w_buf.at[x, zl], w_buf.at[x, zl], win_send.at[i], win_recv.at[i], at_z(d))
        copy.start()
        windows.append(copy)
    xp = remote(
        x_ref.at[:, pl.ds(pl.multiple_of((1 - g) * 4096, 4096), 4096)],
        xp_buf,
        xp_sem.at[0],
        xp_sem.at[1],
        partner,
    )
    xp.start()
    y_att = []
    for i, d in enumerate((1, 3, 2)):
        pair = pl.ds(((y + d) % NY) * 2, 2)
        y_att.append(
            (
                remote(ys_buf.at[pair], ysr_buf.at[i], y_send.at[0, i], y_recv.at[0, i], at_y(d)),
                remote(ya_buf.at[pair], yar_buf.at[i], y_send.at[1, i], y_recv.at[1, i], at_y(d)),
            )
        )
        for copy in y_att[-1]:
            copy.start()

    xp.wait_recv()
    pieces = []
    for other in range(NX):
        columns = pl.ds(pl.multiple_of((g * NX + other) * 1024, 1024), 1024)
        pieces += [x_ref[:, columns], xp_buf[:, other * 1024 : (other + 1) * 1024]]
    picked = jnp.dot(
        jnp.concatenate(pieces, axis=0), sel_mat[...], preferred_element_type=F32
    ).astype(BF16)
    sel_mat[0:128, :] = picked

    for copy in windows:
        copy.wait_recv()

    left, right = (x + NX - 1) % NX, (x + 1) % NX
    across = (x + 2) % NX
    to_right = remote(w_buf.at[x], w_buf.at[x], x_send.at[0], x_recv.at[0], at_x(1))
    to_left = remote(w_buf.at[x], w_buf.at[x], x_send.at[1], x_recv.at[1], at_x(-1))
    to_right.start()
    to_left.start()

    for copies in y_att:
        for copy in copies:
            copy.wait_recv()
    for pair in range(2):
        stats = [ys_buf[y * 2 + pair]] + [ysr_buf[i, pair] for i in range(3)]
        parts = [ya_buf[y * 2 + pair]] + [yar_buf[i, pair] for i in range(3)]
        peak = functools.reduce(jnp.maximum, [s[0:1] for s in stats])
        factors = [jnp.exp(s[0:1] - peak) for s in stats]
        total = sum(s[1:2] * f for s, f in zip(stats, factors))
        part = sum(p.astype(F32) * f for p, f in zip(parts, factors))
        row = lax.broadcasted_iota(jnp.int32, (8, 128), 0)
        zs_buf[pair] = jnp.where(row == 0, peak, total)
        turned = part.T.astype(BF16)
        za_buf[2 * pair] = turned[:64]
        za_buf[2 * pair + 1] = turned[64:]
    z_att = []
    for i, d in enumerate((2, 1, 3)):
        dest = (zh + d) % ZHI
        z_att.append(
            (
                remote(zs_buf.at[dest // 2], zsr_buf.at[i], z_send.at[0, i], z_recv.at[0, i], at_z(8 * d)),
                remote(za_buf.at[dest], zar_buf.at[i], z_send.at[1, i], z_recv.at[1, i], at_z(8 * d)),
            )
        )
        for copy in z_att[-1]:
            copy.start()

    def slab_product(other):
        lhs = sel_mat[pl.ds(pl.multiple_of(other * 32, 32), 32), :]
        lhs = jnp.concatenate([lhs[:, :128], lhs[:, 128:]], axis=0)
        slab = w_buf[other]
        top = jnp.max(jnp.abs(slab.astype(F32)), axis=0)
        return jnp.dot(lhs, slab.reshape(128, 512), preferred_element_type=F32), top

    partial, top = slab_product(x)
    to_right.wait_recv()
    on_right = remote(
        w_buf.at[left, pl.ds(0, 4)], w_buf.at[left, pl.ds(0, 4)], x_send.at[2], x_recv.at[2], at_x(1)
    )
    on_right.start()
    to_left.wait_recv()
    on_left = remote(
        w_buf.at[right, pl.ds(4, 4)], w_buf.at[right, pl.ds(4, 4)], x_send.at[3], x_recv.at[3], at_x(-1)
    )
    on_left.start()
    for other in (left, right):
        more, more_top = slab_product(other)
        partial, top = partial + more, jnp.maximum(top, more_top)
    on_right.wait_recv()
    on_left.wait_recv()
    more, more_top = slab_product(across)
    partial, top = partial + more, jnp.maximum(top, more_top)

    tops = [
        jnp.broadcast_to(jnp.max(top[h * 8 : h * 8 + 8], axis=0, keepdims=True), (8, 512))
        for h in range(2)
    ]
    for h in range(2):
        cs_buf[h, 0:16] = partial[h * 32 + 16 : h * 32 + 32]
        cs_buf[h, 16:24] = tops[h]
    core = remote(cs_buf, cr_buf, c_sem.at[0], c_sem.at[1], partner)
    core.start()
    core.wait_recv()
    for h in range(2):
        both = partial[h * 32 : h * 32 + 16] + cr_buf[h, 0:16]
        highest = jnp.maximum(tops[h], cr_buf[h, 16:24])
        for k in range(2):
            yf_buf[2 * h + k, 0:16] = both[:, k * 256 : (k + 1) * 256]
            yf_buf[2 * h + k, 16:24] = highest[:, k * 256 : (k + 1) * 256]
    y_new = []
    for i, d in enumerate((1, 3, 2)):
        copy = remote(yf_buf.at[(y + d) % NY], yfr_buf.at[i], y_send.at[2, i], y_recv.at[2, i], at_y(d))
        copy.start()
        y_new.append(copy)
    for copy in y_new:
        copy.wait_recv()
    blocks = [yf_buf[y]] + [yfr_buf[i] for i in range(3)]
    added = sum(b[0:16] for b in blocks)
    highest = functools.reduce(jnp.maximum, [b[16:24] for b in blocks])
    for k in range(2):
        zf_buf[k, 0:16] = added[:, k * 128 : (k + 1) * 128]
        zf_buf[k, 16:24] = highest[:, k * 128 : (k + 1) * 128]
    z_new = []
    for i, d in enumerate((2, 1, 3)):
        dest = (zh + d) % ZHI
        copy = remote(zf_buf.at[dest // 2], zfr_buf.at[i], z_send.at[2, i], z_recv.at[2, i], at_z(8 * d))
        copy.start()
        z_new.append(copy)

    head = y * 2 + zh // 2
    own_queries = jnp.concatenate(
        [q_ref[:, pl.ds(pl.multiple_of(head * 1024 + h * 128, 128), 128)] for h in range(8)], axis=0
    )
    own_keys = nk_ref[:, pl.ds(pl.multiple_of(head * 128, 128), 128)]
    new_scores = (
        lax.dot_general(own_keys, own_queries, (((1,), (1,)), ((), ())), preferred_element_type=F32)
        * inverse
    )
    r = lax.broadcasted_iota(jnp.int32, (16, 128), 0)
    c = lax.broadcasted_iota(jnp.int32, (16, 128), 1)
    causal = jnp.logical_and((r & 3) == (c & 3), (r >> 2) <= ((c >> 2) & 3))
    new_scores = jnp.where(causal, new_scores, masked_score)
    new_peak = jnp.max(new_scores, axis=0, keepdims=True)

    for copies in z_att:
        for copy in copies:
            copy.wait_recv()
    stats = [zs_buf[zh // 2]] + [zsr_buf[i] for i in range(3)]
    parts = [za_buf[zh]] + [zar_buf[i] for i in range(3)]
    peak = functools.reduce(jnp.maximum, [s[0:1] for s in stats] + [new_peak])
    factors = [jnp.exp(s[0:1] - peak) for s in stats]
    new_weights = jnp.where(causal, jnp.exp(new_scores - peak), 0.0)
    denominator = sum(s[1:2] * f for s, f in zip(stats, factors)) + jnp.sum(
        new_weights, axis=0, keepdims=True
    )
    share = 1.0 / denominator
    columns = jnp.concatenate([f * share for f in factors] + [share] * 4, axis=0).T
    odd = (zh % 2) == 1
    columns = jnp.where(odd, columns[64:], columns[:64])
    merged = sum(p.astype(F32) * columns[:, i : i + 1] for i, p in enumerate(parts))

    for copy in z_new:
        copy.wait_recv()
    blocks = [zf_buf[zh // 2]] + [zfr_buf[i] for i in range(3)]
    values = sum(b[0:16] for b in blocks).astype(BF16)
    highest = functools.reduce(jnp.maximum, [b[16:24] for b in blocks])
    scales = (highest + scale_floor) / code_range
    scale_ref[...] = jnp.where(odd, scales[:, 64:], scales[:, :64])
    wide = values.astype(F32)
    fresh_ref[...] = jnp.where(odd, wide[:, 64:], wide[:, :64]).astype(BF16)
    mixed = lax.dot_general(
        new_weights.astype(BF16), values, (((0,), (0,)), ((), ())), preferred_element_type=F32
    )
    mixed = jnp.where(odd, mixed[64:], mixed[:64])
    result = merged + mixed * columns[:, 4:5]
    for h in range(4):
        att_ref[:, h * 128 : (h + 1) * 128] = result[h * 16 : (h + 1) * 16]

    for copy in windows + [xp, to_right, to_left, on_right, on_left, core] + y_new + z_new:
        copy.wait_send()
    for copies in y_att + z_att:
        for copy in copies:
            copy.wait_send()


def body(
    master_weight,
    grad,
    moment1,
    moment2,
    step_count,
    x_new,
    queries,
    new_keys,
    cache_keys,
    cache_values,
    lengths,
):
    vmem = pl.BlockSpec(memory_space=pltpu.VMEM)
    smem = pl.BlockSpec(memory_space=pltpu.SMEM)
    dma = pltpu.SemaphoreType.DMA
    new_weight, scale, fresh, attention = pl.pallas_call(
        kernel,
        out_shape=(
            jax.ShapeDtypeStruct((8, 1024), F32),
            jax.ShapeDtypeStruct((8, 64), F32),
            jax.ShapeDtypeStruct((16, 64), BF16),
            jax.ShapeDtypeStruct((16, 512), F32),
        ),
        in_specs=[vmem] * 4 + [smem] + [vmem] * 5 + [smem],
        out_specs=(vmem,) * 4,
        scratch_shapes=[
            pltpu.VMEM((NX, ZLO, 16, 512), BF16),
            pltpu.VMEM((16, 4096), BF16),
            pltpu.VMEM((1024, 256), BF16),
            pltpu.VMEM((256, 128), F32),
            pltpu.VMEM((KV, 128, 128), BF16),
            pltpu.VMEM((KV, 8, 128), F32),
            pltpu.VMEM((3, 2, 128, 128), BF16),
            pltpu.VMEM((3, 2, 8, 128), F32),
            pltpu.VMEM((4, 64, 128), BF16),
            pltpu.VMEM((2, 8, 128), F32),
            pltpu.VMEM((3, 64, 128), BF16),
            pltpu.VMEM((3, 8, 128), F32),
            pltpu.VMEM((2, 24, 512), F32),
            pltpu.VMEM((2, 24, 512), F32),
            pltpu.VMEM((4, 24, 256), F32),
            pltpu.VMEM((3, 24, 256), F32),
            pltpu.VMEM((2, 24, 128), F32),
            pltpu.VMEM((3, 24, 128), F32),
            dma((7,)),
            dma((7,)),
            dma((4,)),
            dma((4,)),
            dma((2,)),
            dma((2,)),
            dma((3, 3)),
            dma((3, 3)),
            dma((3, 3)),
            dma((3, 3)),
        ],
        compiler_params=pltpu.CompilerParams(collective_id=0, has_side_effects=True),
    )(
        master_weight,
        grad,
        moment1,
        moment2,
        step_count,
        x_new.reshape(16, 8192),
        queries.reshape(16, 8192),
        new_keys.reshape(16, 1024),
        cache_keys.reshape(256, 1024),
        cache_values.reshape(256, 1024),
        lengths,
    )
    return (
        new_weight,
        scale[0],
        fresh.reshape(STEPS, BR, 64),
        attention.reshape(STEPS, BR, 512),
    )


def solution(mesh):
    return jax.shard_map(
        body,
        mesh=mesh,
        in_specs=(
            P(("group", "rep", "tp"), None),
            P(("group", "rep", "tp"), None),
            P(("group", "rep", "tp"), None),
            P(("group", "rep", "tp"), None),
            P(),
            P(None, ("group", "rep"), None),
            P(None, ("group", "rep"), None),
            P(None, ("group", "rep"), None),
            P(("group", "rep"), "tp", None),
            P(("group", "rep"), "tp", None),
            P(("group", "rep"), None),
        ),
        out_specs=(
            P(("group", "rep", "tp"), None),
            P("tp"),
            P(None, ("group", "rep"), "tp"),
            P(None, ("group", "rep"), "tp"),
        ),
        check_vma=False,
    )
```

time: 291 us -> 71.7 us (0.25)
  waiting for transfers between devices: 188 us -> 0 us
  starting transfers between devices: 65.2 us -> 0 us
  Pallas kernels: 0 us -> 62.3 us
  between operations: 15.2 us -> 1.29 us
  other arithmetic: 6.69 us -> 0 us
  local copies, waits for them, and re-layouts: 11.3 us -> 7.73 us
    all_to_all x5 -> x0, waiting for transfers between devices: 98.2 us -> none  [the longest x1 26.4 us: body(): lax.all_to_all(sum_local[None], 'tp', split_axis=2, concat_axis=0, tiled=...]
    all_gather x1 -> x0, waiting for transfers between devices: 89.9 us -> none  [body(): gathered = lax.all_gather(moved, ('group', 'rep'), axis=0, tiled=True)]
    all_to_all x5 -> x0, starting transfers between devices: 65.1 us -> none  [the longest x1 31.6 us: body(): lax.all_to_all(new_weight, 'tp', split_axis=1, concat_axis=0, tiled=True)]
    pallas_call x0 -> x1, Pallas kernels: none -> 62.3 us  [body(): pl.pallas_call(kernel, out_shape=(jax.ShapeDtypeStruct((8, 1024), F32), j...]
    reduce_max x2 -> x0, other arithmetic: 3.47 us -> none  [the longest x1 3.43 us: body(): scale_own = (jnp.max(jnp.abs(gathered), axis=0) + scale_floor) / code_range]
    reshape x6 -> x4, local copies, waits for them, and re-layouts: 2.02 us -> 5.28 us  [the longest x1 1.75 us: body(): x_new.reshape(16, 8192)]
    another operation x4 -> x0, local copies, waits for them, and re-layouts: 3.06 us -> none  [the longest x1 1.14 us: body(): part_local[None]]
  transfers between devices with their start and end apart: 6 -> 0, of which waited for: 5 -> 0; matrix products, arithmetic and copies ran while one was open for 5% -> 0% of each run, Pallas kernels for 0% -> 0%
where the time goes in v1:
time: 71.7 us; the launch traced here: 71.3 us
  Pallas kernels  62.3 us (87%)
  local copies, waits for them, and re-layouts  7.73 us (11%)
  between operations  1.29 us (2%)
    pallas_call x1, Pallas kernels, body(): pl.pallas_call(kernel, out_shape=(jax.ShapeDtypeStruct((8, 1024), F32), j...  62.3 us
    reshape x1, local copies, waits for them, and re-layouts, body(): x_new.reshape(16, 8192)  1.75 us

profile of v1, /device:TPU:1, one launch (start us, length us, event | category | flops | bytes accessed | tf_op | source)
XLA Modules:
  0.0 71.3 jit_solution(2662085284683765950)
XLA Ops:
  1.3 1.4 %reshape.31.nk_ref = bf16[16,1024]{1,0:T(8,128)(2,1)} reshape(bf16[4,4,1024]{2,1,0:T(4,128)(2,1)} %param.18) | data formatting | bytes 65536 | tf_op jit(solution)/shard_map/reshape | solution.py:431
  2.7 0.0 copy-start
  2.7 1.7 %reshape.29.x_ref = bf16[16,8192]{1,0:T(8,128)(2,1)} reshape(bf16[4,4,8192]{2,1,0:T(4,128)(2,1)} %param.16) | data formatting | bytes 524288 | tf_op jit(solution)/shard_map/reshape | solution.py:429
  4.4 0.0 copy-done
  4.4 0.8 %reshape.30.q_ref = bf16[16,8192]{1,0:T(8,128)(2,1)} reshape(bf16[4,4,8192]{2,1,0:T(4,128)(2,1)S(1)} %copy-done) | data formatting | bytes 524288 | tf_op jit(solution)/shard_map/reshape | solution.py:430
  5.2 62.3 %shard_map.138 = (f32[8,1024]{1,0:T(8,128)}, f32[8,64]{1,0:T(8,128)}, bf16[16,64]{1,0:T(8,128)(2,1)}, f32[16,512]{1,0:T(8,128)}) custom-call(f32[8,1024]{1,0:T(8,128)} %mw_ref.1, f32[8,1024]{1,0:T(8,128)} %grad_ref.1, f32[8,1024]{1,0:T(8,128)} %m1_ref.1, f32[8,1024]{1,0:T(8,128)} %m2_ref.1, s32[1]{0:T(128)S(6)} %copy.17.step_ref, ...), custom_call_target="tpu_custom_call" | custom-call | tf_op jit(solution)/shard_map/pallas_call | solution.py:382
  67.4 1.2 %slice_bitcast_fusion = f32[64]{0:T(128)} fusion(f32[8,64]{1,0:T(8,128)} %get-tuple-element.9), kind=kLoop, calls=%fused_computation | loop fusion | bytes 512 | tf_op jit(solution)/shard_map/squeeze | solution.py:438
  68.6 0.0 copy-start.1
  68.6 1.4 %reshape.35 = f32[4,4,512]{2,1,0:T(4,128)} reshape(f32[16,512]{1,0:T(8,128)} %get-tuple-element.11) | data formatting | bytes 65536 | tf_op jit(solution)/shard_map/reshape | solution.py:440
  70.0 0.0 copy-done.1
  70.0 0.0 copy-start.2
  70.0 0.6 copy.18
  70.6 0.1 copy-done.2
  70.7 0.6 copy.19
Async XLA Ops:
  2.7 1.8 %copy-start = (bf16[4,4,8192]{2,1,0:T(4,128)(2,1)S(1)}, bf16[4,4,8192]{2,1,0:T(4,128)(2,1)}, u32[]{:S(2)}) copy-start(bf16[4,4,8192]{2,1,0:T(4,128)(2,1)} %param.17) | copy-start | bytes 786436
  68.6 1.4 %copy-start.1 = (f32[8,1024]{1,0:T(8,128)S(1)}, f32[8,1024]{1,0:T(8,128)}, u32[]{:S(2)}) copy-start(f32[8,1024]{1,0:T(8,128)} %get-tuple-element.16) | copy-start | bytes 98308
  70.0 0.7 copy-start.2

commit v2 on v1

v2 whole, which is shorter than its diff:
```python
import functools
import math

import jax
import jax.numpy as jnp
from jax import lax
from jax.experimental import pallas as pl
from jax.experimental.pallas import tpu as pltpu
from jax.sharding import PartitionSpec as P

H = 64
KV = 8
HD = 128
STEPS = 4
BR = 4

beta_first = 0.9
beta_second = 0.999
learn_rate = 0.01
decay_rate = 0.1
adam_floor = 1e-08
scale_floor = 1e-06
code_range = 448.0
masked_score = -1e30

F32 = jnp.float32
BF16 = jnp.bfloat16
MESH = pl.DeviceIdType.MESH

NX, NY, ZLO, ZHI = 4, 4, 8, 4
NZ = ZLO * ZHI
SOURCES = (0, -1, 1, -2, 2, -3, 3, -4)


def adamw(mw, grad, m1, m2, step):
    steps_done = jnp.full(mw.shape, step, jnp.int32).astype(F32)
    first = beta_first * m1 + (1.0 - beta_first) * grad
    second = beta_second * m2 + (1.0 - beta_second) * grad * grad
    correction = jnp.sqrt(1.0 - jnp.exp(steps_done * math.log(beta_second))) / (
        1.0 - jnp.exp(steps_done * math.log(beta_first))
    )
    return mw - learn_rate * correction * first / (jnp.sqrt(second) + adam_floor) - learn_rate * decay_rate * mw


def kernel(
    mw_hbm,
    grad_hbm,
    m1_hbm,
    m2_hbm,
    step_ref,
    x_hbm,
    q_hbm,
    nk_hbm,
    k_hbm,
    v_hbm,
    len_ref,
    scale_ref,
    fresh_ref,
    att_ref,
    rows_buf,
    x4_buf,
    q4_buf,
    nk4_buf,
    k_ref,
    v_ref,
    xf_buf,
    q_ref,
    w_buf,
    xp_buf,
    sel_mat,
    pick_buf,
    mask_buf,
    ya_buf,
    ys_buf,
    yar_buf,
    ysr_buf,
    za_buf,
    zs_buf,
    zar_buf,
    zsr_buf,
    cs_buf,
    cr_buf,
    yf_buf,
    yfr_buf,
    zf_buf,
    zfr_buf,
    zm_buf,
    zmr_buf,
    in_sem,
    win_send,
    win_recv,
    x_send,
    x_recv,
    xp_sem,
    c_sem,
    y_send,
    y_recv,
    z_send,
    z_recv,
    hello,
):
    g = lax.axis_index("group")
    rep = lax.axis_index("rep")
    tp = lax.axis_index("tp")
    x, zl = rep // ZLO, rep % ZLO
    y, zh = tp // ZHI, tp % ZHI
    z = zh * ZLO + zl

    def at_z(offset):
        there = (z + offset + NZ) % NZ
        return {"rep": x * ZLO + there % ZLO, "tp": y * ZHI + there // ZLO}

    def at_x(offset):
        return {"rep": ((x + offset + NX) % NX) * ZLO + zl}

    def at_y(offset):
        return {"tp": ((y + offset) % NY) * ZHI + zh}

    partner = {"group": 1 - g}

    def signal(sem, peer):
        pl.semaphore_signal(sem, inc=1, device_id=peer, device_id_type=MESH)

    def remote(src, dst, send, recv, peer):
        return pltpu.make_async_remote_copy(
            src_ref=src, dst_ref=dst, send_sem=send, recv_sem=recv, device_id=peer, device_id_type=MESH
        )

    barrier = pltpu.get_barrier_semaphore()
    peers = [at_z(d) for d in (4, -4, 3, -3, 2, -2, 1, -1)]
    peers += [at_y(d) for d in (2, 1, 3)] + [at_x(d) for d in (1, -1)] + [partner]
    for peer in peers:
        signal(barrier, peer)

    loads = [
        pltpu.make_async_copy(src, dst, in_sem.at[i])
        for i, (src, dst) in enumerate(
            [(ref, rows_buf.at[i]) for i, ref in enumerate((mw_hbm, grad_hbm, m1_hbm, m2_hbm))]
            + [(q_hbm, q4_buf), (k_hbm, k_ref), (v_hbm, v_ref), (x_hbm, x4_buf), (nk_hbm, nk4_buf)]
        )
    ]
    for copy in loads:
        copy.start()

    for copy in loads[:4]:
        copy.wait()
    nw = adamw(rows_buf[0], rows_buf[1], rows_buf[2], rows_buf[3], step_ref[0])
    w_buf[x, zl] = jnp.concatenate([nw[:, :512], nw[:, 512:]], axis=0).astype(BF16)

    pl.semaphore_wait(barrier, len(peers))

    windows = [None]
    for i, e in enumerate(SOURCES):
        if e:
            own = w_buf.at[x, zl]
            copy = remote(own, own, win_send.at[i], win_recv.at[i], at_z(-e))
            copy.start()
            windows.append(copy)
    sent = []
    left, right, across = (x + NX - 1) % NX, (x + 1) % NX, (x + 2) % NX
    from_left, from_right, from_across = {}, {}, {}

    def block(owner, i):
        return w_buf.at[owner, (zl + SOURCES[i] + ZLO) % ZLO]

    def spread(i):
        ref = block(x, i)
        from_left[i] = remote(ref, ref, x_send.at[0, i], x_recv.at[0, i], at_x(1))
        from_right[i] = remote(ref, ref, x_send.at[1, i], x_recv.at[1, i], at_x(-1))
        from_left[i].start()
        from_right[i].start()

    def pass_on(i):
        from_left[i].wait_recv()
        from_right[i].wait_recv()
        if i % 2 == 0:
            ref = block(left, i)
            copy = remote(ref, ref, x_send.at[2, i], x_recv.at[2, i], at_x(1))
        else:
            ref = block(right, i)
            copy = remote(ref, ref, x_send.at[2, i], x_recv.at[2, i], at_x(-1))
        copy.start()
        from_across[i] = copy

    spread(0)
    half = pl.ds(pl.multiple_of((1 - g) * 4096, 4096), 4096)
    xp = remote(x_hbm.at[:, :, half], xp_buf, xp_sem.at[0], xp_sem.at[1], partner)
    xp.start()
    signal(hello.at[0], at_z(4))
    signal(hello.at[1], at_z(-4))

    rows_b = []
    lane_b = lax.broadcasted_iota(jnp.int32, (64, 128), 1) & 3
    position = tp * 64 + lax.broadcasted_iota(jnp.int32, (64, 128), 0)
    for b in range(BR):
        live = jnp.logical_and(position < len_ref[0, b], lane_b == b)
        rows_b.append(jnp.where(live, 1.0, 0.0))
    mask_buf[...] = jnp.concatenate(rows_b, axis=0)
    inverse = 1.0 / math.sqrt(HD)
    loads[4].wait()
    for s in range(STEPS):
        q_ref[4 * s : 4 * s + 4] = q4_buf[s].astype(F32)

    def head_queries(kv):
        return jnp.concatenate(
            [q_ref[:, pl.ds(pl.multiple_of(kv * 1024 + h * 128, 128), 128)] for h in range(8)], axis=0
        ).astype(BF16)

    def attend(kv, carry):
        columns = pl.ds(pl.multiple_of(kv * 128, 128), 128)
        scores = (
            lax.dot_general(
                k_ref[:, columns], head_queries(kv), (((1,), (1,)), ((), ())), preferred_element_type=F32
            )
            * inverse
        )
        live = mask_buf[...] > 0.5
        masked = jnp.where(live, scores, masked_score)
        peak = jnp.max(masked, axis=0, keepdims=True)
        weights = jnp.where(live, jnp.exp(masked - peak), 0.0)
        total = jnp.sum(weights, axis=0, keepdims=True)
        part = lax.dot_general(
            v_ref[:, columns],
            weights.astype(BF16),
            (((0,), (0,)), ((), ())),
            preferred_element_type=F32,
        )
        ya_buf[kv] = part.astype(BF16)
        ys_buf[kv] = jnp.concatenate([peak, total], axis=0)
        return carry

    loads[5].wait()
    loads[6].wait()
    lax.fori_loop(0, KV // 2, attend, 0)
    for i in (1, 2, 3):
        windows[i].wait_recv()
        spread(i)
    lax.fori_loop(KV // 2, KV, attend, 0)
    y_att = []
    for i, d in enumerate((1, 3, 2)):
        pair = pl.ds(((y + d) % NY) * 2, 2)
        y_att.append(
            (
                remote(ys_buf.at[pair], ysr_buf.at[i], y_send.at[0, i], y_recv.at[0, i], at_y(d)),
                remote(ya_buf.at[pair], yar_buf.at[i], y_send.at[1, i], y_recv.at[1, i], at_y(d)),
            )
        )
        for copy in y_att[-1]:
            copy.start()
    for i in (4, 5, 6, 7):
        windows[i].wait_recv()
        spread(i)
    for i in (0, 1, 2):
        pass_on(i)
    pl.semaphore_wait(hello.at[0], 1)
    pl.semaphore_wait(hello.at[1], 1)
    signal(hello.at[2], at_z(8))
    signal(hello.at[3], at_z(-8))

    for low in range(ZLO):
        there = (z + 28 + (low - z + 4 + NZ) % ZLO) % NZ
        lanes = (y * ZHI + there // ZLO) * 8
        r = lax.broadcasted_iota(jnp.int32, (128, 256), 0)
        c = lax.broadcasted_iota(jnp.int32, (128, 256), 1)
        k = c & 127
        hit = jnp.logical_and(
            jnp.logical_and((k >> 4) == low, ((k >> 3) & 1) == (c >> 7)), r == lanes + (k & 7)
        )
        sel_mat[low * 128 : (low + 1) * 128, :] = jnp.where(hit, 1.0, 0.0).astype(BF16)
    loads[7].wait()
    xp.wait_recv()
    for other in range(NX):
        columns = pl.ds(pl.multiple_of((g * NX + other) * 1024, 1024), 1024)
        for s in range(STEPS):
            xf_buf[other * 32 + 4 * s : other * 32 + 4 * s + 4] = x4_buf[s, :, columns].astype(F32)
            xf_buf[other * 32 + 16 + 4 * s : other * 32 + 16 + 4 * s + 4] = xp_buf[
                s, :, other * 1024 : (other + 1) * 1024
            ].astype(F32)
    pick_buf[...] = jnp.dot(xf_buf[...].astype(BF16), sel_mat[...], preferred_element_type=F32)

    def slab_product(owner):
        lhs = pick_buf[pl.ds(pl.multiple_of(owner * 32, 32), 32), :].astype(BF16)
        lhs = jnp.concatenate([lhs[:, :128], lhs[:, 128:]], axis=0)
        slab = w_buf[owner]
        top = jnp.max(jnp.abs(slab.astype(F32)), axis=0)
        return jnp.dot(lhs, slab.reshape(128, 512), preferred_element_type=F32), top

    partial, top = slab_product(x)
    for i in (3, 4, 5):
        pass_on(i)

    for copies in y_att:
        for copy in copies:
            copy.wait_recv()
    for pair in range(2):
        stats = [ys_buf[y * 2 + pair]] + [ysr_buf[i, pair] for i in range(3)]
        parts = [ya_buf[y * 2 + pair]] + [yar_buf[i, pair] for i in range(3)]
        peak = functools.reduce(jnp.maximum, [s[0:1] for s in stats])
        factors = [jnp.exp(s[0:1] - peak) for s in stats]
        total = sum(s[1:2] * f for s, f in zip(stats, factors))
        part = sum(p.astype(F32) * f for p, f in zip(parts, factors))
        zs_buf[pair] = jnp.concatenate([peak, total], axis=0)
        turned = part.T.astype(BF16)
        za_buf[2 * pair] = turned[:64]
        za_buf[2 * pair + 1] = turned[64:]
    pl.semaphore_wait(hello.at[2], 1)
    pl.semaphore_wait(hello.at[3], 1)
    z_att = []
    for i, d in enumerate((2, 1, 3)):
        dest = (zh + d) % ZHI
        z_att.append(
            (
                remote(zs_buf.at[dest // 2], zsr_buf.at[i], z_send.at[0, i], z_recv.at[0, i], at_z(8 * d)),
                remote(za_buf.at[dest], zar_buf.at[i], z_send.at[1, i], z_recv.at[1, i], at_z(8 * d)),
            )
        )
        for copy in z_att[-1]:
            copy.start()

    for i in (6, 7):
        pass_on(i)
    for owner in (left, right):
        more, more_top = slab_product(owner)
        partial, top = partial + more, jnp.maximum(top, more_top)
    for i in range(8):
        from_across[i].wait_recv()
    more, more_top = slab_product(across)
    partial, top = partial + more, jnp.maximum(top, more_top)

    tops = [
        jnp.broadcast_to(jnp.max(top[h * 8 : h * 8 + 8], axis=0, keepdims=True), (8, 512))
        for h in range(2)
    ]
    for h in range(2):
        cs_buf[h, 0:16] = partial[h * 32 + 16 : h * 32 + 32]
        cs_buf[h, 16:24] = tops[h]
    core = remote(cs_buf, cr_buf, c_sem.at[0], c_sem.at[1], partner)
    core.start()
    core.wait_recv()
    for h in range(2):
        both = partial[h * 32 : h * 32 + 16] + cr_buf[h, 0:16]
        highest = jnp.maximum(tops[h], cr_buf[h, 16:24])
        for k in range(2):
            yf_buf[2 * h + k, 0:16] = both[:, k * 256 : (k + 1) * 256]
            yf_buf[2 * h + k, 16:24] = highest[:, k * 256 : (k + 1) * 256]
    y_new = []
    for i, d in enumerate((1, 3, 2)):
        copy = remote(yf_buf.at[(y + d) % NY], yfr_buf.at[i], y_send.at[2, i], y_recv.at[2, i], at_y(d))
        copy.start()
        y_new.append(copy)
    for copy in y_new:
        copy.wait_recv()
    blocks = [yf_buf[y]] + [yfr_buf[i] for i in range(3)]
    added = sum(b[0:16] for b in blocks)
    highest = functools.reduce(jnp.maximum, [b[16:17] for b in blocks])
    for k in range(2):
        zf_buf[k] = added[:, k * 128 : (k + 1) * 128].astype(BF16)
        zm_buf[k] = highest[:, k * 128 : (k + 1) * 128]
    z_new = []
    for i, d in enumerate((2, 1, 3)):
        dest = (zh + d) % ZHI
        z_new.append(
            (
                remote(zf_buf.at[dest // 2], zfr_buf.at[i], z_send.at[2, i], z_recv.at[2, i], at_z(8 * d)),
                remote(zm_buf.at[dest // 2], zmr_buf.at[i], z_send.at[3, i], z_recv.at[3, i], at_z(8 * d)),
            )
        )
        for copy in z_new[-1]:
            copy.start()
    mine = jnp.where((zh // 2) == 1, added[:, 128:], added[:, :128])

    head = y * 2 + zh // 2
    loads[8].wait()
    own_keys = jnp.concatenate(
        [nk4_buf[s, :, pl.ds(pl.multiple_of(head * 128, 128), 128)].astype(F32) for s in range(STEPS)], axis=0
    ).astype(BF16)
    new_scores = (
        lax.dot_general(own_keys, head_queries(head), (((1,), (1,)), ((), ())), preferred_element_type=F32)
        * inverse
    )
    r = lax.broadcasted_iota(jnp.int32, (16, 128), 0)
    c = lax.broadcasted_iota(jnp.int32, (16, 128), 1)
    causal = jnp.logical_and((r & 3) == (c & 3), (r >> 2) <= ((c >> 2) & 3))
    new_scores = jnp.where(causal, new_scores, masked_score)
    new_peak = jnp.max(new_scores, axis=0, keepdims=True)

    for copies in z_att:
        for copy in copies:
            copy.wait_recv()
    stats = [zs_buf[zh // 2]] + [zsr_buf[i] for i in range(3)]
    parts = [za_buf[zh]] + [zar_buf[i] for i in range(3)]
    peak = functools.reduce(jnp.maximum, [s[0:1] for s in stats] + [new_peak])
    factors = [jnp.exp(s[0:1] - peak) for s in stats]
    new_weights = jnp.where(causal, jnp.exp(new_scores - peak), 0.0)
    denominator = sum(s[1:2] * f for s, f in zip(stats, factors)) + jnp.sum(
        new_weights, axis=0, keepdims=True
    )
    share = 1.0 / denominator
    columns = jnp.concatenate([f * share for f in factors] + [share] * 4, axis=0).T
    odd = (zh % 2) == 1
    columns = jnp.where(odd, columns[64:], columns[:64])
    merged = sum(p.astype(F32) * columns[:, i : i + 1] for i, p in enumerate(parts))

    for copies in z_new:
        for copy in copies:
            copy.wait_recv()
    values = (mine + sum(zfr_buf[i].astype(F32) for i in range(3))).astype(BF16)
    highest = functools.reduce(jnp.maximum, [zm_buf[zh // 2]] + [zmr_buf[i] for i in range(3)])
    scales = (highest + scale_floor) / code_range
    scale_ref[...] = jnp.broadcast_to(jnp.where(odd, scales[:, 64:], scales[:, :64]), (8, 64))
    wide = values.astype(F32)
    fresh_ref[...] = jnp.where(odd, wide[:, 64:], wide[:, :64])
    mixed = lax.dot_general(
        new_weights.astype(BF16), values, (((0,), (0,)), ((), ())), preferred_element_type=F32
    )
    mixed = jnp.where(odd, mixed[64:], mixed[:64])
    result = merged + mixed * columns[:, 4:5]
    for h in range(4):
        att_ref[:, h * 128 : (h + 1) * 128] = result[h * 16 : (h + 1) * 16]

    for copy in windows[1:] + [xp, core] + y_new:
        copy.wait_send()
    for i in range(8):
        from_left[i].wait_send()
        from_right[i].wait_send()
        from_across[i].wait_send()
    for copies in y_att + z_att + z_new:
        for copy in copies:
            copy.wait_send()


def finish(mw, grad, m1, m2, step, scale, fresh, att, nw_out, scale_out, fresh_out, att_out):
    nw_out[...] = adamw(mw[...], grad[...], m1[...], m2[...], step[0])
    scale_out[...] = scale[0:1]
    for s in range(STEPS):
        fresh_out[s] = fresh[4 * s : 4 * s + 4].astype(BF16)
        att_out[s] = att[4 * s : 4 * s + 4]


def body(
    master_weight,
    grad,
    moment1,
    moment2,
    step_count,
    x_new,
    queries,
    new_keys,
    cache_keys,
    cache_values,
    lengths,
):
    vmem = pl.BlockSpec(memory_space=pltpu.VMEM)
    smem = pl.BlockSpec(memory_space=pltpu.SMEM)
    hbm = pl.BlockSpec(memory_space=pl.ANY)
    dma = pltpu.SemaphoreType.DMA
    optimizer = (master_weight, grad, moment1, moment2, step_count)
    scale, fresh, attention = pl.pallas_call(
        kernel,
        out_shape=(
            jax.ShapeDtypeStruct((8, 64), F32),
            jax.ShapeDtypeStruct((16, 64), F32),
            jax.ShapeDtypeStruct((16, 512), F32),
        ),
        in_specs=[hbm] * 4 + [smem] + [hbm] * 5 + [smem],
        out_specs=(vmem,) * 3,
        scratch_shapes=[
            pltpu.VMEM((4, 8, 1024), F32),
            pltpu.VMEM((STEPS, BR, 8192), BF16),
            pltpu.VMEM((STEPS, BR, 8192), BF16),
            pltpu.VMEM((STEPS, BR, 1024), BF16),
            pltpu.VMEM((256, 1024), BF16),
            pltpu.VMEM((256, 1024), BF16),
            pltpu.VMEM((128, 1024), F32),
            pltpu.VMEM((16, 8192), F32),
            pltpu.VMEM((NX, ZLO, 16, 512), BF16),
            pltpu.VMEM((STEPS, BR, 4096), BF16),
            pltpu.VMEM((1024, 256), BF16),
            pltpu.VMEM((128, 256), F32),
            pltpu.VMEM((256, 128), F32),
            pltpu.VMEM((KV, 128, 128), BF16),
            pltpu.VMEM((KV, 2, 128), F32),
            pltpu.VMEM((3, 2, 128, 128), BF16),
            pltpu.VMEM((3, 2, 2, 128), F32),
            pltpu.VMEM((4, 64, 128), BF16),
            pltpu.VMEM((2, 2, 128), F32),
            pltpu.VMEM((3, 64, 128), BF16),
            pltpu.VMEM((3, 2, 128), F32),
            pltpu.VMEM((2, 24, 512), F32),
            pltpu.VMEM((2, 24, 512), F32),
            pltpu.VMEM((4, 24, 256), F32),
            pltpu.VMEM((3, 24, 256), F32),
            pltpu.VMEM((2, 16, 128), BF16),
            pltpu.VMEM((3, 16, 128), BF16),
            pltpu.VMEM((2, 1, 128), F32),
            pltpu.VMEM((3, 1, 128), F32),
            dma((9,)),
            dma((8,)),
            dma((8,)),
            dma((3, 8)),
            dma((3, 8)),
            dma((2,)),
            dma((2,)),
            dma((3, 3)),
            dma((3, 3)),
            dma((4, 3)),
            dma((4, 3)),
            pltpu.SemaphoreType.REGULAR((4,)),
        ],
        compiler_params=pltpu.CompilerParams(collective_id=0, has_side_effects=True),
    )(
        *optimizer,
        x_new,
        queries,
        new_keys,
        cache_keys.reshape(256, 1024),
        cache_values.reshape(256, 1024),
        lengths,
    )
    new_weight, scale, fresh, attention = pl.pallas_call(
        finish,
        out_shape=(
            jax.ShapeDtypeStruct((8, 1024), F32),
            jax.ShapeDtypeStruct((1, 64), F32),
            jax.ShapeDtypeStruct((STEPS, BR, 64), BF16),
            jax.ShapeDtypeStruct((STEPS, BR, 512), F32),
        ),
        in_specs=[vmem] * 4 + [smem] + [vmem] * 3,
        out_specs=(vmem,) * 4,
    )(*optimizer, scale, fresh, attention)
    return new_weight, scale[0], fresh, attention


def solution(mesh):
    return jax.shard_map(
        body,
        mesh=mesh,
        in_specs=(
            P(("group", "rep", "tp"), None),
            P(("group", "rep", "tp"), None),
            P(("group", "rep", "tp"), None),
            P(("group", "rep", "tp"), None),
            P(),
            P(None, ("group", "rep"), None),
            P(None, ("group", "rep"), None),
            P(None, ("group", "rep"), None),
            P(("group", "rep"), "tp", None),
            P(("group", "rep"), "tp", None),
            P(("group", "rep"), None),
        ),
        out_specs=(
            P(("group", "rep", "tp"), None),
            P("tp"),
            P(None, ("group", "rep"), "tp"),
            P(None, ("group", "rep"), "tp"),
        ),
        check_vma=False,
    )
```

time: 71.7 us -> 61.4 us (0.86)
  local copies, waits for them, and re-layouts: 7.73 us -> 0 us
  Pallas kernels: 62.3 us -> 59.9 us
    reshape x4 -> x0, local copies, waits for them, and re-layouts: 5.28 us -> none  [the longest x1 1.75 us: body(): x_new.reshape(16, 8192)]
    pallas_call x1 -> x2, Pallas kernels: 62.3 us -> 59.9 us  [the longest x1 58.4 us: body(): pl.pallas_call(kernel, out_shape=(jax.ShapeDtypeStruct((8, 64), F32), jax...]
    unnamed x8 -> x0, local copies, waits for them, and re-layouts: 1.28 us -> none
    squeeze x1 -> x0, local copies, waits for them, and re-layouts: 1.17 us -> none  [body(): scale[0]]
where the time goes in v2:
time: 61.4 us; the launch traced here: 61.2 us
  Pallas kernels  59.9 us (98%)
  between operations  1.29 us (2%)
    pallas_call x1, Pallas kernels, body(): pl.pallas_call(kernel, out_shape=(jax.ShapeDtypeStruct((8, 64), F32), jax...  58.4 us
    pallas_call x1, Pallas kernels, body(): pl.pallas_call(finish, out_shape=(jax.ShapeDtypeStruct((8, 1024), F32), j...  1.51 us

profile of v2, /device:TPU:1, one launch (start us, length us, event | category | flops | bytes accessed | tf_op | source)
XLA Modules:
  0.0 61.2 jit_solution(1396512963499790494)
XLA Ops:
  1.3 58.4 %shard_map.138 = (f32[8,64]{1,0:T(8,128)}, f32[16,64]{1,0:T(8,128)}, f32[16,512]{1,0:T(8,128)}) custom-call(f32[8,1024]{1,0:T(8,128)} %mw.1, f32[8,1024]{1,0:T(8,128)} %grad.1, f32[8,1024]{1,0:T(8,128)} %m1.1, f32[8,1024]{1,0:T(8,128)} %m2.1, s32[1]{0:T(128)S(6)} %copy.15.step_ref.step, bf16[4,4,8192]{2,1,0:T(4,128)(2,1)} %x_hbm.1, ...), custom_call_target="tpu_custom_call" | custom-call | tf_op jit(solution)/shard_map/pallas_call | solution.py:458
  59.7 1.5 %shard_map.139 = (f32[8,1024]{1,0:T(8,128)}, f32[1,64]{1,0:T(1,128)}, bf16[4,4,64]{2,1,0:T(4,128)(2,1)}, f32[4,4,512]{2,1,0:T(4,128)}) custom-call(f32[8,1024]{1,0:T(8,128)} %mw.1, f32[8,1024]{1,0:T(8,128)} %grad.1, f32[8,1024]{1,0:T(8,128)} %m1.1, f32[8,1024]{1,0:T(8,128)} %m2.1, s32[1]{0:T(128)S(6)} %copy.15.step_ref.step, ...), custom_call_target="tpu_custom_call" | custom-call | tf_op jit(solution)/shard_map/pallas_call | solution.py:520

commit v3 on v2

--- a/solution.py
+++ b/solution.py
@@ -30,6 +30,14 @@
 NX, NY, ZLO, ZHI = 4, 4, 8, 4
 NZ = ZLO * ZHI
 SOURCES = (0, -1, 1, -2, 2, -3, 3, -4)
+NEAR = tuple(
+    (dx, dy, dg)
+    for far in (4, 3, 2, 1, 0)
+    for dx in range(NX)
+    for dy in range(NY)
+    for dg in range(2)
+    if min(dx, NX - dx) + min(dy, NY - dy) == far and (dx, dy, dg) != (0, 0, 0)
+)
 
 
 def adamw(mw, grad, m1, m2, step):
@@ -66,9 +74,9 @@
     xf_buf,
     q_ref,
     w_buf,
-    xp_buf,
     sel_mat,
-    pick_buf,
+    ps_buf,
+    pr_buf,
     mask_buf,
     ya_buf,
     ys_buf,
@@ -78,10 +86,10 @@
     zs_buf,
     zar_buf,
     zsr_buf,
-    cs_buf,
-    cr_buf,
-    yf_buf,
-    yfr_buf,
+    pd_buf,
+    pdr_buf,
+    pm_buf,
+    pmr_buf,
     zf_buf,
     zfr_buf,
     zm_buf,
@@ -89,10 +97,12 @@
     in_sem,
     win_send,
     win_recv,
-    x_send,
-    x_recv,
-    xp_sem,
-    c_sem,
+    pick_send,
+    pick_recv,
+    d_send,
+    d_recv,
+    m_send,
+    m_recv,
     y_send,
     y_recv,
     z_send,
@@ -110,13 +120,15 @@
         there = (z + offset + NZ) % NZ
         return {"rep": x * ZLO + there % ZLO, "tp": y * ZHI + there // ZLO}
 
-    def at_x(offset):
-        return {"rep": ((x + offset + NX) % NX) * ZLO + zl}
-
     def at_y(offset):
         return {"tp": ((y + offset) % NY) * ZHI + zh}
 
-    partner = {"group": 1 - g}
+    def at_xyg(dx, dy, dg):
+        return {
+            "group": 1 - g if dg else g,
+            "rep": ((x + dx) % NX) * ZLO + zl,
+            "tp": ((y + dy) % NY) * ZHI + zh,
+        }
 
     def signal(sem, peer):
         pl.semaphore_signal(sem, inc=1, device_id=peer, device_id_type=MESH)
@@ -128,7 +140,7 @@
 
     barrier = pltpu.get_barrier_semaphore()
     peers = [at_z(d) for d in (4, -4, 3, -3, 2, -2, 1, -1)]
-    peers += [at_y(d) for d in (2, 1, 3)] + [at_x(d) for d in (1, -1)] + [partner]
+    peers += [at_xyg(*there) for there in NEAR]
     for peer in peers:
         signal(barrier, peer)
 
@@ -142,50 +154,49 @@
     for copy in loads:
         copy.start()
 
+    for low in range(ZLO):
+        there = (z + 28 + (low - z + 4 + NZ) % ZLO) % NZ
+        lanes = (y * ZHI + there // ZLO) * 8
+        r = lax.broadcasted_iota(jnp.int32, (128, 256), 0)
+        c = lax.broadcasted_iota(jnp.int32, (128, 256), 1)
+        k = c & 127
+        hit = jnp.logical_and(
+            jnp.logical_and((k >> 4) == low, ((k >> 3) & 1) == (c >> 7)), r == lanes + (k & 7)
+        )
+        sel_mat[low * 128 : (low + 1) * 128, :] = jnp.where(hit, 1.0, 0.0).astype(BF16)
+
     for copy in loads[:4]:
         copy.wait()
     nw = adamw(rows_buf[0], rows_buf[1], rows_buf[2], rows_buf[3], step_ref[0])
-    w_buf[x, zl] = jnp.concatenate([nw[:, :512], nw[:, 512:]], axis=0).astype(BF16)
+    w_buf[zl] = jnp.concatenate([nw[:, :512], nw[:, 512:]], axis=0).astype(BF16)
 
     pl.semaphore_wait(barrier, len(peers))
 
     windows = [None]
     for i, e in enumerate(SOURCES):
         if e:
-            own = w_buf.at[x, zl]
+            own = w_buf.at[zl]
             copy = remote(own, own, win_send.at[i], win_recv.at[i], at_z(-e))
             copy.start()
             windows.append(copy)
-    sent = []
-    left, right, across = (x + NX - 1) % NX, (x + 1) % NX, (x + 2) % NX
-    from_left, from_right, from_across = {}, {}, {}
-
-    def block(owner, i):
-        return w_buf.at[owner, (zl + SOURCES[i] + ZLO) % ZLO]
-
-    def spread(i):
-        ref = block(x, i)
-        from_left[i] = remote(ref, ref, x_send.at[0, i], x_recv.at[0, i], at_x(1))
-        from_right[i] = remote(ref, ref, x_send.at[1, i], x_recv.at[1, i], at_x(-1))
-        from_left[i].start()
-        from_right[i].start()
-
-    def pass_on(i):
-        from_left[i].wait_recv()
-        from_right[i].wait_recv()
-        if i % 2 == 0:
-            ref = block(left, i)
-            copy = remote(ref, ref, x_send.at[2, i], x_recv.at[2, i], at_x(1))
-        else:
-            ref = block(right, i)
-            copy = remote(ref, ref, x_send.at[2, i], x_recv.at[2, i], at_x(-1))
+    loads[7].wait()
+    for j in range(8):
+        for step in range(STEPS):
+            xf_buf[j * 16 + 4 * step : j * 16 + 4 * step + 4] = x4_buf[
+                step, :, j * 1024 : (j + 1) * 1024
+            ].astype(F32)
+    picked = jnp.dot(xf_buf[...].astype(BF16), sel_mat[...], preferred_element_type=F32).astype(BF16)
+    for j in range(8):
+        ps_buf[j] = picked[j * 16 : (j + 1) * 16]
+    picks = []
+    for dx, dg in ((2, 1), (2, 0), (1, 1), (1, 0), (3, 1), (3, 0), (0, 1)):
+        there = (1 - g if dg else g) * NX + (x + dx) % NX
+        back = ((NX - dx) % NX) * 2 + dg
+        copy = remote(
+            ps_buf.at[there], pr_buf.at[back], pick_send.at[back], pick_recv.at[back], at_xyg(dx, 0, dg)
+        )
         copy.start()
-        from_across[i] = copy
-
-    spread(0)
-    half = pl.ds(pl.multiple_of((1 - g) * 4096, 4096), 4096)
-    xp = remote(x_hbm.at[:, :, half], xp_buf, xp_sem.at[0], xp_sem.at[1], partner)
-    xp.start()
+        picks.append(copy)
     signal(hello.at[0], at_z(4))
     signal(hello.at[1], at_z(-4))
 
@@ -231,11 +242,7 @@
 
     loads[5].wait()
     loads[6].wait()
-    lax.fori_loop(0, KV // 2, attend, 0)
-    for i in (1, 2, 3):
-        windows[i].wait_recv()
-        spread(i)
-    lax.fori_loop(KV // 2, KV, attend, 0)
+    lax.fori_loop(0, KV, attend, 0)
     y_att = []
     for i, d in enumerate((1, 3, 2)):
         pair = pl.ds(((y + d) % NY) * 2, 2)
@@ -247,47 +254,37 @@
         )
         for copy in y_att[-1]:
             copy.start()
-    for i in (4, 5, 6, 7):
-        windows[i].wait_recv()
-        spread(i)
-    for i in (0, 1, 2):
-        pass_on(i)
+    for copy in picks:
+        copy.wait_recv()
+    lhs = jnp.concatenate([ps_buf[g * NX + x]] + [pr_buf[i] for i in range(1, 8)], axis=0)
+    lhs = jnp.concatenate([lhs[:, :128], lhs[:, 128:]], axis=0)
+    for copy in windows[1:]:
+        copy.wait_recv()
+    rows = w_buf[...]
+    product = jnp.dot(lhs, rows.reshape(128, 512), preferred_element_type=F32).astype(BF16)
+    top = jnp.max(jnp.abs(rows.astype(F32)), axis=0)
+    for h in range(2):
+        high = jnp.max(top[h * 8 : h * 8 + 8], axis=0, keepdims=True)
+        for k in range(2):
+            pm_buf[2 * h + k] = high[:, k * 256 : (k + 1) * 256]
+            for i in range(8):
+                first = h * 128 + i * 16
+                pd_buf[i, 2 * h + k] = product[first : first + 16, k * 256 : (k + 1) * 256]
+    direct = []
+    for dx, dy, dg in NEAR:
+        there = (y + dy) % NY
+        back = (((NX - dx) % NX) * NY + (NY - dy) % NY) * 2 + dg
+        peer = at_xyg(dx, dy, dg)
+        direct += [
+            remote(pd_buf.at[dx * 2 + dg, there], pdr_buf.at[back], d_send.at[back], d_recv.at[back], peer),
+            remote(pm_buf.at[there], pmr_buf.at[back], m_send.at[back], m_recv.at[back], peer),
+        ]
+        direct[-2].start()
+        direct[-1].start()
     pl.semaphore_wait(hello.at[0], 1)
     pl.semaphore_wait(hello.at[1], 1)
     signal(hello.at[2], at_z(8))
     signal(hello.at[3], at_z(-8))
-
-    for low in range(ZLO):
-        there = (z + 28 + (low - z + 4 + NZ) % ZLO) % NZ
-        lanes = (y * ZHI + there // ZLO) * 8
-        r = lax.broadcasted_iota(jnp.int32, (128, 256), 0)
-        c = lax.broadcasted_iota(jnp.int32, (128, 256), 1)
-        k = c & 127
-        hit = jnp.logical_and(
-            jnp.logical_and((k >> 4) == low, ((k >> 3) & 1) == (c >> 7)), r == lanes + (k & 7)
-        )
-        sel_mat[low * 128 : (low + 1) * 128, :] = jnp.where(hit, 1.0, 0.0).astype(BF16)
-    loads[7].wait()
-    xp.wait_recv()
-    for other in range(NX):
-        columns = pl.ds(pl.multiple_of((g * NX + other) * 1024, 1024), 1024)
-        for s in range(STEPS):
-            xf_buf[other * 32 + 4 * s : other * 32 + 4 * s + 4] = x4_buf[s, :, columns].astype(F32)
-            xf_buf[other * 32 + 16 + 4 * s : other * 32 + 16 + 4 * s + 4] = xp_buf[
-                s, :, other * 1024 : (other + 1) * 1024
-            ].astype(F32)
-    pick_buf[...] = jnp.dot(xf_buf[...].astype(BF16), sel_mat[...], preferred_element_type=F32)
-
-    def slab_product(owner):
-        lhs = pick_buf[pl.ds(pl.multiple_of(owner * 32, 32), 32), :].astype(BF16)
-        lhs = jnp.concatenate([lhs[:, :128], lhs[:, 128:]], axis=0)
-        slab = w_buf[owner]
-        top = jnp.max(jnp.abs(slab.astype(F32)), axis=0)
-        return jnp.dot(lhs, slab.reshape(128, 512), preferred_element_type=F32), top
-
-    partial, top = slab_product(x)
-    for i in (3, 4, 5):
-        pass_on(i)
 
     for copies in y_att:
         for copy in copies:
@@ -317,42 +314,10 @@
         for copy in z_att[-1]:
             copy.start()
 
-    for i in (6, 7):
-        pass_on(i)
-    for owner in (left, right):
-        more, more_top = slab_product(owner)
-        partial, top = partial + more, jnp.maximum(top, more_top)
-    for i in range(8):
-        from_across[i].wait_recv()
-    more, more_top = slab_product(across)
-    partial, top = partial + more, jnp.maximum(top, more_top)
-
-    tops = [
-        jnp.broadcast_to(jnp.max(top[h * 8 : h * 8 + 8], axis=0, keepdims=True), (8, 512))
-        for h in range(2)
-    ]
-    for h in range(2):
-        cs_buf[h, 0:16] = partial[h * 32 + 16 : h * 32 + 32]
-        cs_buf[h, 16:24] = tops[h]
-    core = remote(cs_buf, cr_buf, c_sem.at[0], c_sem.at[1], partner)
-    core.start()
-    core.wait_recv()
-    for h in range(2):
-        both = partial[h * 32 : h * 32 + 16] + cr_buf[h, 0:16]
-        highest = jnp.maximum(tops[h], cr_buf[h, 16:24])
-        for k in range(2):
-            yf_buf[2 * h + k, 0:16] = both[:, k * 256 : (k + 1) * 256]
-            yf_buf[2 * h + k, 16:24] = highest[:, k * 256 : (k + 1) * 256]
-    y_new = []
-    for i, d in enumerate((1, 3, 2)):
-        copy = remote(yf_buf.at[(y + d) % NY], yfr_buf.at[i], y_send.at[2, i], y_recv.at[2, i], at_y(d))
-        copy.start()
-        y_new.append(copy)
-    for copy in y_new:
+    for copy in direct:
         copy.wait_recv()
-    blocks = [yf_buf[y]] + [yfr_buf[i] for i in range(3)]
-    added = sum(b[0:16] for b in blocks)
-    highest = functools.reduce(jnp.maximum, [b[16:17] for b in blocks])
+    added = pd_buf[0, y].astype(F32) + sum(pdr_buf[i].astype(F32) for i in range(1, 32))
+    highest = functools.reduce(jnp.maximum, [pm_buf[y]] + [pmr_buf[i] for i in range(1, 32)])
     for k in range(2):
         zf_buf[k] = added[:, k * 128 : (k + 1) * 128].astype(BF16)
         zm_buf[k] = highest[:, k * 128 : (k + 1) * 128]
@@ -418,12 +383,8 @@
     for h in range(4):
         att_ref[:, h * 128 : (h + 1) * 128] = result[h * 16 : (h + 1) * 16]
 
-    for copy in windows[1:] + [xp, core] + y_new:
+    for copy in windows[1:] + picks + direct:
         copy.wait_send()
-    for i in range(8):
-        from_left[i].wait_send()
-        from_right[i].wait_send()
-        from_across[i].wait_send()
     for copies in y_att + z_att + z_new:
         for copy in copies:
             copy.wait_send()
@@ -473,10 +434,10 @@
             pltpu.VMEM((256, 1024), BF16),
             pltpu.VMEM((128, 1024), F32),
             pltpu.VMEM((16, 8192), F32),
-            pltpu.VMEM((NX, ZLO, 16, 512), BF16),
-            pltpu.VMEM((STEPS, BR, 4096), BF16),
+            pltpu.VMEM((ZLO, 16, 512), BF16),
             pltpu.VMEM((1024, 256), BF16),
-            pltpu.VMEM((128, 256), F32),
+            pltpu.VMEM((8, 16, 256), BF16),
+            pltpu.VMEM((8, 16, 256), BF16),
             pltpu.VMEM((256, 128), F32),
             pltpu.VMEM((KV, 128, 128), BF16),
             pltpu.VMEM((KV, 2, 128), F32),
@@ -486,10 +447,10 @@
             pltpu.VMEM((2, 2, 128), F32),
             pltpu.VMEM((3, 64, 128), BF16),
             pltpu.VMEM((3, 2, 128), F32),
-            pltpu.VMEM((2, 24, 512), F32),
-            pltpu.VMEM((2, 24, 512), F32),
-            pltpu.VMEM((4, 24, 256), F32),
-            pltpu.VMEM((3, 24, 256), F32),
+            pltpu.VMEM((8, NY, 16, 256), BF16),
+            pltpu.VMEM((32, 16, 256), BF16),
+            pltpu.VMEM((NY, 1, 256), F32),
+            pltpu.VMEM((32, 1, 256), F32),
             pltpu.VMEM((2, 16, 128), BF16),
             pltpu.VMEM((3, 16, 128), BF16),
             pltpu.VMEM((2, 1, 128), F32),
@@ -497,10 +458,12 @@
             dma((9,)),
             dma((8,)),
             dma((8,)),
-            dma((3, 8)),
-            dma((3, 8)),
-            dma((2,)),
-            dma((2,)),
+            dma((8,)),
+            dma((8,)),
+            dma((32,)),
+            dma((32,)),
+            dma((32,)),
+            dma((32,)),
             dma((3, 3)),
             dma((3, 3)),
             dma((4, 3)),

time: 61.4 us -> 57 us (0.928)
  the two profiles are of different devices: /device:TPU:1 before, /device:TPU:32 now
where the time goes in v3:
time: 57 us; the launch traced here: 56.7 us
  Pallas kernels  55.5 us (97%)
  between operations  1.29 us (2%)
    pallas_call x1, Pallas kernels, body(): pl.pallas_call(kernel, out_shape=(jax.ShapeDtypeStruct((8, 64), F32), jax...  53.9 us
    pallas_call x1, Pallas kernels, body(): pl.pallas_call(finish, out_shape=(jax.ShapeDtypeStruct((8, 1024), F32), j...  1.51 us

profile of v3, /device:TPU:32, one launch (start us, length us, event | category | flops | bytes accessed | tf_op | source)
XLA Modules:
  0.0 56.7 jit_solution(16006938065331811905)
XLA Ops:
  1.3 53.9 %shard_map.138 = (f32[8,64]{1,0:T(8,128)}, f32[16,64]{1,0:T(8,128)}, f32[16,512]{1,0:T(8,128)}) custom-call(f32[8,1024]{1,0:T(8,128)} %mw.1, f32[8,1024]{1,0:T(8,128)} %grad.1, f32[8,1024]{1,0:T(8,128)} %m1.1, f32[8,1024]{1,0:T(8,128)} %m2.1, s32[1]{0:T(128)S(6)} %copy.15.step_ref.step, bf16[4,4,8192]{2,1,0:T(4,128)(2,1)} %x_hbm.1, ...), custom_call_target="tpu_custom_call" | custom-call | tf_op jit(solution)/shard_map/pallas_call | solution.py:419
  55.2 1.5 %shard_map.139 = (f32[8,1024]{1,0:T(8,128)}, f32[1,64]{1,0:T(1,128)}, bf16[4,4,64]{2,1,0:T(4,128)(2,1)}, f32[4,4,512]{2,1,0:T(4,128)}) custom-call(f32[8,1024]{1,0:T(8,128)} %mw.1, f32[8,1024]{1,0:T(8,128)} %grad.1, f32[8,1024]{1,0:T(8,128)} %m1.1, f32[8,1024]{1,0:T(8,128)} %m2.1, s32[1]{0:T(128)S(6)} %copy.15.step_ref.step, ...), custom_call_target="tpu_custom_call" | custom-call | tf_op jit(solution)/shard_map/pallas_call | solution.py:483

commit v4 on v3

--- a/solution.py
+++ b/solution.py
@@ -29,7 +29,7 @@
 
 NX, NY, ZLO, ZHI = 4, 4, 8, 4
 NZ = ZLO * ZHI
-SOURCES = (0, -1, 1, -2, 2, -3, 3, -4)
+SOURCES = (-4, 3, -3, 2, -2, 1, -1)
 NEAR = tuple(
     (dx, dy, dg)
     for far in (4, 3, 2, 1, 0)
@@ -107,6 +107,8 @@
     y_recv,
     z_send,
     z_recv,
+    n_send,
+    n_recv,
     hello,
 ):
     g = lax.axis_index("group")
@@ -123,11 +125,12 @@
     def at_y(offset):
         return {"tp": ((y + offset) % NY) * ZHI + zh}
 
-    def at_xyg(dx, dy, dg):
+    def at_xyg(dx, dy, dg, dz=0):
+        there = (z + dz + NZ) % NZ
         return {
             "group": 1 - g if dg else g,
-            "rep": ((x + dx) % NX) * ZLO + zl,
-            "tp": ((y + dy) % NY) * ZHI + zh,
+            "rep": ((x + dx) % NX) * ZLO + there % ZLO,
+            "tp": ((y + dy) % NY) * ZHI + there // ZLO,
         }
 
     def signal(sem, peer):
@@ -140,6 +143,7 @@
 
     barrier = pltpu.get_barrier_semaphore()
     peers = [at_z(d) for d in (4, -4, 3, -3, 2, -2, 1, -1)]
+    peers += [at_xyg(dx, 0, dg, dz) for dz in (4, -4) for dx in range(NX) for dg in range(2) if dx or dg]
     peers += [at_xyg(*there) for there in NEAR]
     for peer in peers:
         signal(barrier, peer)
@@ -155,15 +159,16 @@
         copy.start()
 
     for low in range(ZLO):
-        there = (z + 28 + (low - z + 4 + NZ) % ZLO) % NZ
-        lanes = (y * ZHI + there // ZLO) * 8
-        r = lax.broadcasted_iota(jnp.int32, (128, 256), 0)
-        c = lax.broadcasted_iota(jnp.int32, (128, 256), 1)
-        k = c & 127
-        hit = jnp.logical_and(
-            jnp.logical_and((k >> 4) == low, ((k >> 3) & 1) == (c >> 7)), r == lanes + (k & 7)
-        )
-        sel_mat[low * 128 : (low + 1) * 128, :] = jnp.where(hit, 1.0, 0.0).astype(BF16)
+        r = lax.broadcasted_iota(jnp.int32, (128, 128), 0)
+        k = lax.broadcasted_iota(jnp.int32, (128, 128), 1)
+        for way in range(2):
+            base = z + (0 if way == 0 else NZ - 8)
+            there = (base + (low - base + 2 * NZ) % ZLO) % NZ
+            lanes = (y * ZHI + there // ZLO) * 8
+            hit = jnp.logical_and((k >> 4) == low, r == lanes + (k & 7))
+            sel_mat[low * 128 : (low + 1) * 128, way * 128 : (way + 1) * 128] = jnp.where(
+                hit, 1.0, 0.0
+            ).astype(BF16)
 
     for copy in loads[:4]:
         copy.wait()
@@ -172,13 +177,14 @@
 
     pl.semaphore_wait(barrier, len(peers))
 
-    windows = [None]
+    signal(hello.at[0], at_z(4))
+    signal(hello.at[1], at_z(-4))
+    windows = []
     for i, e in enumerate(SOURCES):
-        if e:
-            own = w_buf.at[zl]
-            copy = remote(own, own, win_send.at[i], win_recv.at[i], at_z(-e))
-            copy.start()
-            windows.append(copy)
+        own = w_buf.at[zl]
+        copy = remote(own, own, win_send.at[i], win_recv.at[i], at_z(-e))
+        copy.start()
+        windows.append(copy)
     loads[7].wait()
     for j in range(8):
         for step in range(STEPS):
@@ -187,18 +193,21 @@
             ].astype(F32)
     picked = jnp.dot(xf_buf[...].astype(BF16), sel_mat[...], preferred_element_type=F32).astype(BF16)
     for j in range(8):
-        ps_buf[j] = picked[j * 16 : (j + 1) * 16]
+        for way in range(2):
+            ps_buf[way, j] = picked[j * 16 : (j + 1) * 16, way * 128 : (way + 1) * 128]
     picks = []
-    for dx, dg in ((2, 1), (2, 0), (1, 1), (1, 0), (3, 1), (3, 0), (0, 1)):
+    for dx, dg in ((2, 0), (2, 1), (1, 0), (1, 1), (3, 0), (3, 1), (0, 0), (0, 1)):
         there = (1 - g if dg else g) * NX + (x + dx) % NX
         back = ((NX - dx) % NX) * 2 + dg
         copy = remote(
-            ps_buf.at[there], pr_buf.at[back], pick_send.at[back], pick_recv.at[back], at_xyg(dx, 0, dg)
+            ps_buf.at[dg, there],
+            pr_buf.at[back],
+            pick_send.at[back],
+            pick_recv.at[back],
+            at_xyg(dx, 0, dg, -4 if dg else 4),
         )
         copy.start()
         picks.append(copy)
-    signal(hello.at[0], at_z(4))
-    signal(hello.at[1], at_z(-4))
 
     rows_b = []
     lane_b = lax.broadcasted_iota(jnp.int32, (64, 128), 1) & 3
@@ -242,7 +251,12 @@
 
     loads[5].wait()
     loads[6].wait()
-    lax.fori_loop(0, KV, attend, 0)
+    lax.fori_loop(0, KV // 2, attend, 0)
+    pl.semaphore_wait(hello.at[0], 1)
+    pl.semaphore_wait(hello.at[1], 1)
+    signal(hello.at[2], at_z(8))
+    signal(hello.at[3], at_z(-8))
+    lax.fori_loop(KV // 2, KV, attend, 0)
     y_att = []
     for i, d in enumerate((1, 3, 2)):
         pair = pl.ds(((y + d) % NY) * 2, 2)
@@ -256,9 +270,10 @@
             copy.start()
     for copy in picks:
         copy.wait_recv()
-    lhs = jnp.concatenate([ps_buf[g * NX + x]] + [pr_buf[i] for i in range(1, 8)], axis=0)
-    lhs = jnp.concatenate([lhs[:, :128], lhs[:, 128:]], axis=0)
-    for copy in windows[1:]:
+    lhs = pr_buf[...].reshape(128, 128).astype(F32)
+    upper = (lax.broadcasted_iota(jnp.int32, (128, 128), 1) & 8) == 0
+    lhs = jnp.concatenate([jnp.where(upper, lhs, 0.0), jnp.where(upper, 0.0, lhs)], axis=0).astype(BF16)
+    for copy in windows:
         copy.wait_recv()
     rows = w_buf[...]
     product = jnp.dot(lhs, rows.reshape(128, 512), preferred_element_type=F32).astype(BF16)
@@ -281,10 +296,6 @@
         ]
         direct[-2].start()
         direct[-1].start()
-    pl.semaphore_wait(hello.at[0], 1)
-    pl.semaphore_wait(hello.at[1], 1)
-    signal(hello.at[2], at_z(8))
-    signal(hello.at[3], at_z(-8))
 
     for copies in y_att:
         for copy in copies:
@@ -322,17 +333,16 @@
         zf_buf[k] = added[:, k * 128 : (k + 1) * 128].astype(BF16)
         zm_buf[k] = highest[:, k * 128 : (k + 1) * 128]
     z_new = []
-    for i, d in enumerate((2, 1, 3)):
-        dest = (zh + d) % ZHI
+    for i, d in enumerate((12, -12, 4, -4)):
+        half = ((z + d + NZ) % NZ) // 16
         z_new.append(
             (
-                remote(zf_buf.at[dest // 2], zfr_buf.at[i], z_send.at[2, i], z_recv.at[2, i], at_z(8 * d)),
-                remote(zm_buf.at[dest // 2], zmr_buf.at[i], z_send.at[3, i], z_recv.at[3, i], at_z(8 * d)),
+                remote(zf_buf.at[half], zfr_buf.at[i], n_send.at[0, i], n_recv.at[0, i], at_z(d)),
+                remote(zm_buf.at[half], zmr_buf.at[i], n_send.at[1, i], n_recv.at[1, i], at_z(d)),
             )
         )
         for copy in z_new[-1]:
             copy.start()
-    mine = jnp.where((zh // 2) == 1, added[:, 128:], added[:, :128])
 
     head = y * 2 + zh // 2
     loads[8].wait()
@@ -369,8 +379,8 @@
     for copies in z_new:
         for copy in copies:
             copy.wait_recv()
-    values = (mine + sum(zfr_buf[i].astype(F32) for i in range(3))).astype(BF16)
-    highest = functools.reduce(jnp.maximum, [zm_buf[zh // 2]] + [zmr_buf[i] for i in range(3)])
+    values = sum(zfr_buf[i].astype(F32) for i in range(4)).astype(BF16)
+    highest = functools.reduce(jnp.maximum, [zmr_buf[i] for i in range(4)])
     scales = (highest + scale_floor) / code_range
     scale_ref[...] = jnp.broadcast_to(jnp.where(odd, scales[:, 64:], scales[:, :64]), (8, 64))
     wide = values.astype(F32)
@@ -383,7 +393,7 @@
     for h in range(4):
         att_ref[:, h * 128 : (h + 1) * 128] = result[h * 16 : (h + 1) * 16]
 
-    for copy in windows[1:] + picks + direct:
+    for copy in windows + picks + direct:
         copy.wait_send()
     for copies in y_att + z_att + z_new:
         for copy in copies:
@@ -436,8 +446,8 @@
             pltpu.VMEM((16, 8192), F32),
             pltpu.VMEM((ZLO, 16, 512), BF16),
             pltpu.VMEM((1024, 256), BF16),
-            pltpu.VMEM((8, 16, 256), BF16),
-            pltpu.VMEM((8, 16, 256), BF16),
+            pltpu.VMEM((2, 8, 16, 128), BF16),
+            pltpu.VMEM((8, 16, 128), BF16),
             pltpu.VMEM((256, 128), F32),
             pltpu.VMEM((KV, 128, 128), BF16),
             pltpu.VMEM((KV, 2, 128), F32),
@@ -452,9 +462,9 @@
             pltpu.VMEM((NY, 1, 256), F32),
             pltpu.VMEM((32, 1, 256), F32),
             pltpu.VMEM((2, 16, 128), BF16),
-            pltpu.VMEM((3, 16, 128), BF16),
+            pltpu.VMEM((4, 16, 128), BF16),
             pltpu.VMEM((2, 1, 128), F32),
-            pltpu.VMEM((3, 1, 128), F32),
+            pltpu.VMEM((4, 1, 128), F32),
             dma((9,)),
             dma((8,)),
             dma((8,)),
@@ -466,8 +476,10 @@
             dma((32,)),
             dma((3, 3)),
             dma((3, 3)),
-            dma((4, 3)),
-            dma((4, 3)),
+            dma((2, 3)),
+            dma((2, 3)),
+            dma((2, 4)),
+            dma((2, 4)),
             pltpu.SemaphoreType.REGULAR((4,)),
         ],
         compiler_params=pltpu.CompilerParams(collective_id=0, has_side_effects=True),

time: 57 us -> 54.7 us (0.960)
  the two profiles are of different devices: /device:TPU:32 before, /device:TPU:1 now
where the time goes in v4:
time: 54.7 us; the launch traced here: 54.4 us
  Pallas kernels  53.1 us (97%)
  between operations  1.29 us (2%)
    pallas_call x1, Pallas kernels, body(): pl.pallas_call(kernel, out_shape=(jax.ShapeDtypeStruct((8, 64), F32), jax...  51.6 us
    pallas_call x1, Pallas kernels, body(): pl.pallas_call(finish, out_shape=(jax.ShapeDtypeStruct((8, 1024), F32), j...  1.51 us

profile of v4, /device:TPU:1, one launch (start us, length us, event | category | flops | bytes accessed | tf_op | source)
XLA Modules:
  0.0 54.4 jit_solution(1590253970216804530)
XLA Ops:
  1.3 51.6 %shard_map.138 = (f32[8,64]{1,0:T(8,128)}, f32[16,64]{1,0:T(8,128)}, f32[16,512]{1,0:T(8,128)}) custom-call(f32[8,1024]{1,0:T(8,128)} %mw.1, f32[8,1024]{1,0:T(8,128)} %grad.1, f32[8,1024]{1,0:T(8,128)} %m1.1, f32[8,1024]{1,0:T(8,128)} %m2.1, s32[1]{0:T(128)S(6)} %copy.15.step_ref.step, bf16[4,4,8192]{2,1,0:T(4,128)(2,1)} %x_hbm.1, ...), custom_call_target="tpu_custom_call" | custom-call | tf_op jit(solution)/shard_map/pallas_call | solution.py:429
  52.9 1.5 %shard_map.139 = (f32[8,1024]{1,0:T(8,128)}, f32[1,64]{1,0:T(1,128)}, bf16[4,4,64]{2,1,0:T(4,128)(2,1)}, f32[4,4,512]{2,1,0:T(4,128)}) custom-call(f32[8,1024]{1,0:T(8,128)} %mw.1, f32[8,1024]{1,0:T(8,128)} %grad.1, f32[8,1024]{1,0:T(8,128)} %m1.1, f32[8,1024]{1,0:T(8,128)} %m2.1, s32[1]{0:T(128)S(6)} %copy.15.step_ref.step, ...), custom_call_target="tpu_custom_call" | custom-call | tf_op jit(solution)/shard_map/pallas_call | solution.py:495

commit v5 on v4

--- a/solution.py
+++ b/solution.py
@@ -114,24 +114,29 @@
     g = lax.axis_index("group")
     rep = lax.axis_index("rep")
     tp = lax.axis_index("tp")
-    x, zl = rep // ZLO, rep % ZLO
-    y, zh = tp // ZHI, tp % ZHI
+    x, zl = rep >> 3, rep & 7
+    y, zh = tp >> 2, tp & 3
     z = zh * ZLO + zl
+    cores = (g, 1 - g)
+    xs = [(x + d) & 3 for d in range(NX)]
+    ys = [(y + d) & 3 for d in range(NY)]
+    plane_rep = [v * ZLO + zl for v in xs]
+    plane_tp = [v * ZHI + zh for v in ys]
+    zs = {d: (z + d) & 31 for d in (1, 2, 3, 4, 8, 12, 16, 24, -1, -2, -3, -4, -8, -12)}
+    z_rep = {d: x * ZLO + (v & 7) for d, v in zs.items()}
+    z_tp = {d: y * ZHI + (v >> 3) for d, v in zs.items()}
 
     def at_z(offset):
-        there = (z + offset + NZ) % NZ
-        return {"rep": x * ZLO + there % ZLO, "tp": y * ZHI + there // ZLO}
+        return (g, z_rep[offset], z_tp[offset])
 
     def at_y(offset):
-        return {"tp": ((y + offset) % NY) * ZHI + zh}
-
-    def at_xyg(dx, dy, dg, dz=0):
-        there = (z + dz + NZ) % NZ
-        return {
-            "group": 1 - g if dg else g,
-            "rep": ((x + dx) % NX) * ZLO + there % ZLO,
-            "tp": ((y + dy) % NY) * ZHI + there // ZLO,
-        }
+        return (g, rep, plane_tp[offset])
+
+    def at_xyg(dx, dy, dg):
+        return (cores[dg], plane_rep[dx], plane_tp[dy])
+
+    def at_xzg(dx, dz, dg):
+        return (cores[dg], xs[dx] * ZLO + (zs[dz] & 7), z_tp[dz])
 
     def signal(sem, peer):
         pl.semaphore_signal(sem, inc=1, device_id=peer, device_id_type=MESH)
@@ -143,7 +148,6 @@
 
     barrier = pltpu.get_barrier_semaphore()
     peers = [at_z(d) for d in (4, -4, 3, -3, 2, -2, 1, -1)]
-    peers += [at_xyg(dx, 0, dg, dz) for dz in (4, -4) for dx in range(NX) for dg in range(2) if dx or dg]
     peers += [at_xyg(*there) for there in NEAR]
     for peer in peers:
         signal(barrier, peer)
@@ -163,8 +167,8 @@
         k = lax.broadcasted_iota(jnp.int32, (128, 128), 1)
         for way in range(2):
             base = z + (0 if way == 0 else NZ - 8)
-            there = (base + (low - base + 2 * NZ) % ZLO) % NZ
-            lanes = (y * ZHI + there // ZLO) * 8
+            there = (base + ((low - base + 2 * NZ) & 7)) & 31
+            lanes = (y * ZHI + (there >> 3)) * 8
             hit = jnp.logical_and((k >> 4) == low, r == lanes + (k & 7))
             sel_mat[low * 128 : (low + 1) * 128, way * 128 : (way + 1) * 128] = jnp.where(
                 hit, 1.0, 0.0
@@ -175,16 +179,6 @@
     nw = adamw(rows_buf[0], rows_buf[1], rows_buf[2], rows_buf[3], step_ref[0])
     w_buf[zl] = jnp.concatenate([nw[:, :512], nw[:, 512:]], axis=0).astype(BF16)
 
-    pl.semaphore_wait(barrier, len(peers))
-
-    signal(hello.at[0], at_z(4))
-    signal(hello.at[1], at_z(-4))
-    windows = []
-    for i, e in enumerate(SOURCES):
-        own = w_buf.at[zl]
-        copy = remote(own, own, win_send.at[i], win_recv.at[i], at_z(-e))
-        copy.start()
-        windows.append(copy)
     loads[7].wait()
     for j in range(8):
         for step in range(STEPS):
@@ -195,20 +189,21 @@
     for j in range(8):
         for way in range(2):
             ps_buf[way, j] = picked[j * 16 : (j + 1) * 16, way * 128 : (way + 1) * 128]
-    picks = []
-    for dx, dg in ((2, 0), (2, 1), (1, 0), (1, 1), (3, 0), (3, 1), (0, 0), (0, 1)):
-        there = (1 - g if dg else g) * NX + (x + dx) % NX
-        back = ((NX - dx) % NX) * 2 + dg
-        copy = remote(
-            ps_buf.at[dg, there],
-            pr_buf.at[back],
-            pick_send.at[back],
-            pick_recv.at[back],
-            at_xyg(dx, 0, dg, -4 if dg else 4),
-        )
+
+    pl.semaphore_wait(barrier, len(peers))
+
+    signal(hello.at[0], at_z(4))
+    signal(hello.at[1], at_z(-4))
+    for dx in range(NX):
+        for dg in range(2):
+            if dx or dg:
+                signal(hello.at[4], at_xyg(dx, 0, dg))
+    windows = []
+    for i, e in enumerate(SOURCES):
+        own = w_buf.at[zl]
+        copy = remote(own, own, win_send.at[i], win_recv.at[i], at_z(-e))
         copy.start()
-        picks.append(copy)
-
+        windows.append(copy)
     rows_b = []
     lane_b = lax.broadcasted_iota(jnp.int32, (64, 128), 1) & 3
     position = tp * 64 + lax.broadcasted_iota(jnp.int32, (64, 128), 0)
@@ -221,6 +216,21 @@
     for s in range(STEPS):
         q_ref[4 * s : 4 * s + 4] = q4_buf[s].astype(F32)
 
+    pl.semaphore_wait(hello.at[4], 7)
+    picks = []
+    for dx, dg in ((2, 0), (2, 1), (1, 0), (1, 1), (3, 0), (3, 1), (0, 0), (0, 1)):
+        there = cores[dg] * NX + xs[dx]
+        back = ((NX - dx) % NX) * 2 + dg
+        copy = remote(
+            ps_buf.at[dg, there],
+            pr_buf.at[back],
+            pick_send.at[back],
+            pick_recv.at[back],
+            at_xzg(dx, -4 if dg else 4, dg),
+        )
+        copy.start()
+        picks.append(copy)
+
     def head_queries(kv):
         return jnp.concatenate(
             [q_ref[:, pl.ds(pl.multiple_of(kv * 1024 + h * 128, 128), 128)] for h in range(8)], axis=0
@@ -259,7 +269,7 @@
     lax.fori_loop(KV // 2, KV, attend, 0)
     y_att = []
     for i, d in enumerate((1, 3, 2)):
-        pair = pl.ds(((y + d) % NY) * 2, 2)
+        pair = pl.ds(ys[d] * 2, 2)
         y_att.append(
             (
                 remote(ys_buf.at[pair], ysr_buf.at[i], y_send.at[0, i], y_recv.at[0, i], at_y(d)),
@@ -277,25 +287,29 @@
         copy.wait_recv()
     rows = w_buf[...]
     product = jnp.dot(lhs, rows.reshape(128, 512), preferred_element_type=F32).astype(BF16)
+    for i in range(8):
+        for h in range(2):
+            for k in range(2):
+                first = h * 128 + i * 16
+                pd_buf[i, 2 * h + k] = product[first : first + 16, k * 256 : (k + 1) * 256]
+    backs = [(((NX - dx) % NX) * NY + (NY - dy) % NY) * 2 + dg for dx, dy, dg in NEAR]
+    direct = []
+    for (dx, dy, dg), back in zip(NEAR, backs):
+        source = pd_buf.at[dx * 2 + dg, ys[dy]]
+        copy = remote(source, pdr_buf.at[back], d_send.at[back], d_recv.at[back], at_xyg(dx, dy, dg))
+        copy.start()
+        direct.append(copy)
     top = jnp.max(jnp.abs(rows.astype(F32)), axis=0)
     for h in range(2):
         high = jnp.max(top[h * 8 : h * 8 + 8], axis=0, keepdims=True)
         for k in range(2):
             pm_buf[2 * h + k] = high[:, k * 256 : (k + 1) * 256]
-            for i in range(8):
-                first = h * 128 + i * 16
-                pd_buf[i, 2 * h + k] = product[first : first + 16, k * 256 : (k + 1) * 256]
-    direct = []
-    for dx, dy, dg in NEAR:
-        there = (y + dy) % NY
-        back = (((NX - dx) % NX) * NY + (NY - dy) % NY) * 2 + dg
-        peer = at_xyg(dx, dy, dg)
-        direct += [
-            remote(pd_buf.at[dx * 2 + dg, there], pdr_buf.at[back], d_send.at[back], d_recv.at[back], peer),
-            remote(pm_buf.at[there], pmr_buf.at[back], m_send.at[back], m_recv.at[back], peer),
-        ]
-        direct[-2].start()
-        direct[-1].start()
+    for (dx, dy, dg), back in zip(NEAR, backs):
+        copy = remote(
+            pm_buf.at[ys[dy]], pmr_buf.at[back], m_send.at[back], m_recv.at[back], at_xyg(dx, dy, dg)
+        )
+        copy.start()
+        direct.append(copy)
 
     for copies in y_att:
         for copy in copies:
@@ -315,10 +329,10 @@
     pl.semaphore_wait(hello.at[3], 1)
     z_att = []
     for i, d in enumerate((2, 1, 3)):
-        dest = (zh + d) % ZHI
+        dest = (zh + d) & 3
         z_att.append(
             (
-                remote(zs_buf.at[dest // 2], zsr_buf.at[i], z_send.at[0, i], z_recv.at[0, i], at_z(8 * d)),
+                remote(zs_buf.at[dest >> 1], zsr_buf.at[i], z_send.at[0, i], z_recv.at[0, i], at_z(8 * d)),
                 remote(za_buf.at[dest], zar_buf.at[i], z_send.at[1, i], z_recv.at[1, i], at_z(8 * d)),
             )
         )
@@ -334,7 +348,7 @@
         zm_buf[k] = highest[:, k * 128 : (k + 1) * 128]
     z_new = []
     for i, d in enumerate((12, -12, 4, -4)):
-        half = ((z + d + NZ) % NZ) // 16
+        half = zs[d] >> 4
         z_new.append(
             (
                 remote(zf_buf.at[half], zfr_buf.at[i], n_send.at[0, i], n_recv.at[0, i], at_z(d)),
@@ -344,7 +358,7 @@
         for copy in z_new[-1]:
             copy.start()
 
-    head = y * 2 + zh // 2
+    head = y * 2 + (zh >> 1)
     loads[8].wait()
     own_keys = jnp.concatenate(
         [nk4_buf[s, :, pl.ds(pl.multiple_of(head * 128, 128), 128)].astype(F32) for s in range(STEPS)], axis=0
@@ -362,7 +376,7 @@
     for copies in z_att:
         for copy in copies:
             copy.wait_recv()
-    stats = [zs_buf[zh // 2]] + [zsr_buf[i] for i in range(3)]
+    stats = [zs_buf[zh >> 1]] + [zsr_buf[i] for i in range(3)]
     parts = [za_buf[zh]] + [zar_buf[i] for i in range(3)]
     peak = functools.reduce(jnp.maximum, [s[0:1] for s in stats] + [new_peak])
     factors = [jnp.exp(s[0:1] - peak) for s in stats]
@@ -372,7 +386,7 @@
     )
     share = 1.0 / denominator
     columns = jnp.concatenate([f * share for f in factors] + [share] * 4, axis=0).T
-    odd = (zh % 2) == 1
+    odd = (zh & 1) == 1
     columns = jnp.where(odd, columns[64:], columns[:64])
     merged = sum(p.astype(F32) * columns[:, i : i + 1] for i, p in enumerate(parts))
 
@@ -480,7 +494,7 @@
             dma((2, 3)),
             dma((2, 4)),
             dma((2, 4)),
-            pltpu.SemaphoreType.REGULAR((4,)),
+            pltpu.SemaphoreType.REGULAR((5,)),
         ],
         compiler_params=pltpu.CompilerParams(collective_id=0, has_side_effects=True),
     )(

time: 54.7 us -> 55.4 us (1.013)
  Pallas kernels: 53.1 us -> 53.8 us
    pallas_call x1, Pallas kernels: 51.6 us -> 52.3 us  [body(): pl.pallas_call(kernel, out_shape=(jax.ShapeDtypeStruct((8, 64), F32), jax...]
where the time goes in v5:
time: 55.4 us; the launch traced here: 55.1 us
  Pallas kernels  53.8 us (97%)
  between operations  1.29 us (2%)
    pallas_call x1, Pallas kernels, body(): pl.pallas_call(kernel, out_shape=(jax.ShapeDtypeStruct((8, 64), F32), jax...  52.3 us
    pallas_call x1, Pallas kernels, body(): pl.pallas_call(finish, out_shape=(jax.ShapeDtypeStruct((8, 1024), F32), j...  1.51 us

profile of v5, /device:TPU:1, one launch (start us, length us, event | category | flops | bytes accessed | tf_op | source)
XLA Modules:
  0.0 55.1 jit_solution(3339592566512646006)
XLA Ops:
  1.3 52.3 %shard_map.138 = (f32[8,64]{1,0:T(8,128)}, f32[16,64]{1,0:T(8,128)}, f32[16,512]{1,0:T(8,128)}) custom-call(f32[8,1024]{1,0:T(8,128)} %mw.1, f32[8,1024]{1,0:T(8,128)} %grad.1, f32[8,1024]{1,0:T(8,128)} %m1.1, f32[8,1024]{1,0:T(8,128)} %m2.1, s32[1]{0:T(128)S(6)} %copy.15.step_ref.step, bf16[4,4,8192]{2,1,0:T(4,128)(2,1)} %x_hbm.1, ...), custom_call_target="tpu_custom_call" | custom-call | tf_op jit(solution)/shard_map/pallas_call | solution.py:443
  53.6 1.5 %shard_map.139 = (f32[8,1024]{1,0:T(8,128)}, f32[1,64]{1,0:T(1,128)}, bf16[4,4,64]{2,1,0:T(4,128)(2,1)}, f32[4,4,512]{2,1,0:T(4,128)}) custom-call(f32[8,1024]{1,0:T(8,128)} %mw.1, f32[8,1024]{1,0:T(8,128)} %grad.1, f32[8,1024]{1,0:T(8,128)} %m1.1, f32[8,1024]{1,0:T(8,128)} %m2.1, s32[1]{0:T(128)S(6)} %copy.15.step_ref.step, ...), custom_call_target="tpu_custom_call" | custom-call | tf_op jit(solution)/shard_map/pallas_call | solution.py:509

commit v6 on v5

--- a/solution.py
+++ b/solution.py
@@ -41,7 +41,7 @@
 
 
 def adamw(mw, grad, m1, m2, step):
-    steps_done = jnp.full(mw.shape, step, jnp.int32).astype(F32)
+    steps_done = jnp.broadcast_to(step.astype(F32), mw.shape)
     first = beta_first * m1 + (1.0 - beta_first) * grad
     second = beta_second * m2 + (1.0 - beta_second) * grad * grad
     correction = jnp.sqrt(1.0 - jnp.exp(steps_done * math.log(beta_second))) / (
@@ -55,16 +55,18 @@
     grad_hbm,
     m1_hbm,
     m2_hbm,
-    step_ref,
+    step_hbm,
     x_hbm,
     q_hbm,
     nk_hbm,
     k_hbm,
     v_hbm,
-    len_ref,
+    len_hbm,
     scale_ref,
     fresh_ref,
     att_ref,
+    step_ref,
+    len_ref,
     rows_buf,
     x4_buf,
     q4_buf,
@@ -157,6 +159,7 @@
         for i, (src, dst) in enumerate(
             [(ref, rows_buf.at[i]) for i, ref in enumerate((mw_hbm, grad_hbm, m1_hbm, m2_hbm))]
             + [(q_hbm, q4_buf), (k_hbm, k_ref), (v_hbm, v_ref), (x_hbm, x4_buf), (nk_hbm, nk4_buf)]
+            + [(step_hbm, step_ref), (len_hbm, len_ref)]
         )
     ]
     for copy in loads:
@@ -174,9 +177,9 @@
                 hit, 1.0, 0.0
             ).astype(BF16)
 
-    for copy in loads[:4]:
+    for copy in loads[:4] + [loads[9]]:
         copy.wait()
-    nw = adamw(rows_buf[0], rows_buf[1], rows_buf[2], rows_buf[3], step_ref[0])
+    nw = adamw(rows_buf[0], rows_buf[1], rows_buf[2], rows_buf[3], step_ref[...])
     w_buf[zl] = jnp.concatenate([nw[:, :512], nw[:, 512:]], axis=0).astype(BF16)
 
     loads[7].wait()
@@ -204,6 +207,7 @@
         copy = remote(own, own, win_send.at[i], win_recv.at[i], at_z(-e))
         copy.start()
         windows.append(copy)
+    loads[10].wait()
     rows_b = []
     lane_b = lax.broadcasted_iota(jnp.int32, (64, 128), 1) & 3
     position = tp * 64 + lax.broadcasted_iota(jnp.int32, (64, 128), 0)
@@ -415,7 +419,7 @@
 
 
 def finish(mw, grad, m1, m2, step, scale, fresh, att, nw_out, scale_out, fresh_out, att_out):
-    nw_out[...] = adamw(mw[...], grad[...], m1[...], m2[...], step[0])
+    nw_out[...] = adamw(mw[...], grad[...], m1[...], m2[...], step[...])
     scale_out[...] = scale[0:1]
     for s in range(STEPS):
         fresh_out[s] = fresh[4 * s : 4 * s + 4].astype(BF16)
@@ -436,20 +440,21 @@
     lengths,
 ):
     vmem = pl.BlockSpec(memory_space=pltpu.VMEM)
-    smem = pl.BlockSpec(memory_space=pltpu.SMEM)
     hbm = pl.BlockSpec(memory_space=pl.ANY)
     dma = pltpu.SemaphoreType.DMA
-    optimizer = (master_weight, grad, moment1, moment2, step_count)
+    optimizer = (master_weight, grad, moment1, moment2, step_count.reshape(1, 1))
     scale, fresh, attention = pl.pallas_call(
         kernel,
         out_shape=(
-            jax.ShapeDtypeStruct((8, 64), F32),
-            jax.ShapeDtypeStruct((16, 64), F32),
-            jax.ShapeDtypeStruct((16, 512), F32),
+            pltpu.VMEM((8, 64), F32),
+            pltpu.VMEM((16, 64), F32),
+            pltpu.VMEM((16, 512), F32),
         ),
-        in_specs=[hbm] * 4 + [smem] + [hbm] * 5 + [smem],
+        in_specs=[hbm] * 11,
         out_specs=(vmem,) * 3,
         scratch_shapes=[
+            pltpu.VMEM((1, 1), jnp.int32),
+            pltpu.SMEM((1, 4), jnp.int32),
             pltpu.VMEM((4, 8, 1024), F32),
             pltpu.VMEM((STEPS, BR, 8192), BF16),
             pltpu.VMEM((STEPS, BR, 8192), BF16),
@@ -479,7 +484,7 @@
             pltpu.VMEM((4, 16, 128), BF16),
             pltpu.VMEM((2, 1, 128), F32),
             pltpu.VMEM((4, 1, 128), F32),
-            dma((9,)),
+            dma((11,)),
             dma((8,)),
             dma((8,)),
             dma((8,)),
@@ -514,9 +519,9 @@
             jax.ShapeDtypeStruct((STEPS, BR, 64), BF16),
             jax.ShapeDtypeStruct((STEPS, BR, 512), F32),
         ),
-        in_specs=[vmem] * 4 + [smem] + [vmem] * 3,
+        in_specs=[vmem] * 8,
         out_specs=(vmem,) * 4,
-    )(*optimizer, scale, fresh, attention)
+    )(*optimizer, *(pltpu.with_memory_space_constraint(a, pltpu.VMEM) for a in (scale, fresh, attention)))
     return new_weight, scale[0], fresh, attention
 
 

time: 55.4 us -> 54.1 us (0.977)
  Pallas kernels: 53.8 us -> 52.5 us
    pallas_call x1, Pallas kernels: 52.3 us -> 51 us  [body(): pl.pallas_call(kernel, out_shape=(pltpu.VMEM((8, 64), F32), pltpu.VMEM((1...]
where the time goes in v6:
time: 54.1 us; the launch traced here: 53.8 us
  Pallas kernels  52.5 us (97%)
  between operations  1.29 us (2%)
    pallas_call x1, Pallas kernels, body(): pl.pallas_call(kernel, out_shape=(pltpu.VMEM((8, 64), F32), pltpu.VMEM((1...  51 us
    pallas_call x1, Pallas kernels, body(): pl.pallas_call(finish, out_shape=(jax.ShapeDtypeStruct((8, 1024), F32), j...  1.53 us

profile of v6, /device:TPU:1, one launch (start us, length us, event | category | flops | bytes accessed | tf_op | source)
XLA Modules:
  0.0 53.8 jit_solution(13347398382701084864)
XLA Ops:
  1.3 51.0 %shard_map.138 = (f32[8,64]{1,0:T(8,128)S(1)}, f32[16,64]{1,0:T(8,128)S(1)}, f32[16,512]{1,0:T(8,128)S(1)}) custom-call(f32[8,1024]{1,0:T(8,128)} %mw.1, f32[8,1024]{1,0:T(8,128)} %grad.1, f32[8,1024]{1,0:T(8,128)} %m1.1, f32[8,1024]{1,0:T(8,128)} %m2.1, s32[1,1]{1,0:T(1,128)} %bitcast.4.step_hbm, bf16[4,4,8192]{2,1,0:T(4,128)(2,1)} %x_hbm.1, ...), custom_call_target="tpu_custom_call" | custom-call | tf_op jit(solution)/shard_map/pallas_call | solution.py:446
  52.3 1.5 %shard_map.139 = (f32[8,1024]{1,0:T(8,128)}, f32[1,64]{1,0:T(1,128)}, bf16[4,4,64]{2,1,0:T(4,128)(2,1)}, f32[4,4,512]{2,1,0:T(4,128)}) custom-call(f32[8,1024]{1,0:T(8,128)} %mw.1, f32[8,1024]{1,0:T(8,128)} %grad.1, f32[8,1024]{1,0:T(8,128)} %m1.1, f32[8,1024]{1,0:T(8,128)} %m2.1, s32[1,1]{1,0:T(1,128)} %bitcast.5.step, ...), custom_call_target="tpu_custom_call" | custom-call | tf_op jit(solution)/shard_map/pallas_call | solution.py:514

commit v7 on v6

--- a/solution.py
+++ b/solution.py
@@ -62,6 +62,7 @@
     k_hbm,
     v_hbm,
     len_hbm,
+    nw_ref,
     scale_ref,
     fresh_ref,
     att_ref,
@@ -180,6 +181,7 @@
     for copy in loads[:4] + [loads[9]]:
         copy.wait()
     nw = adamw(rows_buf[0], rows_buf[1], rows_buf[2], rows_buf[3], step_ref[...])
+    nw_ref[...] = nw
     w_buf[zl] = jnp.concatenate([nw[:, :512], nw[:, 512:]], axis=0).astype(BF16)
 
     loads[7].wait()
@@ -418,8 +420,8 @@
             copy.wait_send()
 
 
-def finish(mw, grad, m1, m2, step, scale, fresh, att, nw_out, scale_out, fresh_out, att_out):
-    nw_out[...] = adamw(mw[...], grad[...], m1[...], m2[...], step[...])
+def finish(nw, scale, fresh, att, nw_out, scale_out, fresh_out, att_out):
+    nw_out[...] = nw[...]
     scale_out[...] = scale[0:1]
     for s in range(STEPS):
         fresh_out[s] = fresh[4 * s : 4 * s + 4].astype(BF16)
@@ -443,15 +445,16 @@
     hbm = pl.BlockSpec(memory_space=pl.ANY)
     dma = pltpu.SemaphoreType.DMA
     optimizer = (master_weight, grad, moment1, moment2, step_count.reshape(1, 1))
-    scale, fresh, attention = pl.pallas_call(
+    new_weight, scale, fresh, attention = pl.pallas_call(
         kernel,
         out_shape=(
+            pltpu.VMEM((8, 1024), F32),
             pltpu.VMEM((8, 64), F32),
             pltpu.VMEM((16, 64), F32),
             pltpu.VMEM((16, 512), F32),
         ),
         in_specs=[hbm] * 11,
-        out_specs=(vmem,) * 3,
+        out_specs=(vmem,) * 4,
         scratch_shapes=[
             pltpu.VMEM((1, 1), jnp.int32),
             pltpu.SMEM((1, 4), jnp.int32),
@@ -519,9 +522,9 @@
             jax.ShapeDtypeStruct((STEPS, BR, 64), BF16),
             jax.ShapeDtypeStruct((STEPS, BR, 512), F32),
         ),
-        in_specs=[vmem] * 8,
+        in_specs=[vmem] * 4,
         out_specs=(vmem,) * 4,
-    )(*optimizer, *(pltpu.with_memory_space_constraint(a, pltpu.VMEM) for a in (scale, fresh, attention)))
+    )(*(pltpu.with_memory_space_constraint(a, pltpu.VMEM) for a in (new_weight, scale, fresh, attention)))
     return new_weight, scale[0], fresh, attention
 
 

time: 54.1 us -> 53.1 us (0.982)
  Pallas kernels: 52.5 us -> 51.6 us
    pallas_call x1, Pallas kernels: 1.53 us -> 0.64 us  [body(): pl.pallas_call(finish, out_shape=(jax.ShapeDtypeStruct((8, 1024), F32), j...]
where the time goes in v7:
time: 53.1 us; the launch traced here: 52.9 us
  Pallas kernels  51.6 us (97%)
  between operations  1.29 us (2%)
    pallas_call x1, Pallas kernels, body(): pl.pallas_call(kernel, out_shape=(pltpu.VMEM((8, 1024), F32), pltpu.VMEM(...  51 us

profile of v7, /device:TPU:1, one launch (start us, length us, event | category | flops | bytes accessed | tf_op | source)
XLA Modules:
  0.0 52.9 jit_solution(7350379278552571214)
XLA Ops:
  1.3 51.0 %shard_map.138 = (f32[8,1024]{1,0:T(8,128)S(1)}, f32[8,64]{1,0:T(8,128)S(1)}, f32[16,64]{1,0:T(8,128)S(1)}, f32[16,512]{1,0:T(8,128)S(1)}) custom-call(f32[8,1024]{1,0:T(8,128)} %mw_hbm.1, f32[8,1024]{1,0:T(8,128)} %grad_hbm.1, f32[8,1024]{1,0:T(8,128)} %m1_hbm.1, f32[8,1024]{1,0:T(8,128)} %m2_hbm.1, s32[1,1]{1,0:T(1,128)} %bitcast.4.step_hbm, ...), custom_call_target="tpu_custom_call" | custom-call | tf_op jit(solution)/shard_map/pallas_call | solution.py:448
  52.3 0.6 %shard_map.139 = (f32[8,1024]{1,0:T(8,128)}, f32[1,64]{1,0:T(1,128)}, bf16[4,4,64]{2,1,0:T(4,128)(2,1)}, f32[4,4,512]{2,1,0:T(4,128)}) custom-call(f32[8,1024]{1,0:T(8,128)S(1)} %get-tuple-element.12.nw, f32[8,64]{1,0:T(8,128)S(1)} %get-tuple-element.13.scale, f32[16,64]{1,0:T(8,128)S(1)} %get-tuple-element.14.fresh, f32[16,512]{1,0:T(8,128)S(1)} %get-tuple-element.15.att), custom_call_target="tpu_custom_call" | custom-call | tf_op jit(solution)/shard_map/pallas_call | solution.py:517
